TPU v7x, 128 devices: a whole 4x4x4 slice. The times are simulated.
128 devices in a mesh: freq: 64 (over y, x, z_lo, core), grid: 2 (over z_hi).
Axes of the slice: x: 4, y: 4, z: 4 (z_hi: 2, z_lo: 2; z = z_hi * 2 + z_lo), core: 2. Of those that a mesh axis runs over, the one named last changes fastest.
Arguments:
- cross_spectra: float32 [2, 128, 256, 256], P(None, None, 'freq', 'grid'), as said below
- sensor_modes: float32 [128, 96, 256], P('freq', None, 'grid'), may hold values from -0.375 to 0.375
- source_modes: float32 [128, 96, 256], P('freq', None, 'grid'), may hold values from -6 to 6
- wavenumber: float32 [128, 96], P('freq'), may hold values from 0.5 to 2
- attenuation: float32 [128, 96], P('freq'), may hold values from 0.002 to 0.03
- mode_counts: int32 [128], P('freq'), may hold values from 48 to 96
Outputs:
- bartlett_power: float32 [64, 256], P('freq', 'grid')
Inputs may be any that keep to these rules, and one draw needn't show every extreme that they name: `cross_spectra`: each bin's matrix K_f is Hermitian and positive definite. Modes with index mode_counts[f] or more are left out in bin f.
All inputs are finite; a program needn't handle non-finite values.
Results may differ from a plain program's by a relative error of at most 0.0003.
Values sent between devices are 32-bit elements; how exact they have to be, the bound alone decides.
No kernel may reach another device: no remote copies, remote signals or barrier semaphores. Data moves between devices by JAX's collectives and lax.ppermute only.
A program may use at most 128 MiB of HBM per device.

v0:
```python
import jax
import jax.numpy as jnp
from jax import lax
from jax.sharding import PartitionSpec as P

RANGES = 64


HIGH = lax.Precision.HIGHEST


def cut_along(value, dim, length):
    before, after = (value.shape[:dim], value.shape[dim + 1 :])
    return jnp.moveaxis(value.reshape(*before, length, -1, *after), dim, 0)


def laid_out(pieces, dim):
    shape = list(pieces.shape[1:])
    shape[dim] *= pieces.shape[0]
    return jnp.moveaxis(pieces, 0, dim).reshape(shape)


def one_exchange(value, axis, axes, splits, concats):
    sizes = [lax.axis_size(a) for a in axes]
    pieces = cut_along(value, splits[0], sizes[0])
    pieces = jnp.moveaxis(cut_along(pieces, splits[1] + 1, sizes[1]), 0, 1)
    inside = pieces.shape[2:]
    pieces = pieces.reshape(-1, *inside)
    pieces = lax.all_to_all(pieces, axis, split_axis=0, concat_axis=0, tiled=True)
    pieces = laid_out(pieces.reshape(*sizes, *inside), concats[0] + 1)
    return laid_out(pieces, concats[1])


def sent_to_all(value, axis):
    copies = jnp.broadcast_to(value, (lax.axis_size(axis), *value.shape))
    return lax.all_to_all(copies, axis, split_axis=0, concat_axis=0, tiled=True)


def collect(value, axis, dim):
    pieces = sent_to_all(value, axis)
    return laid_out(pieces, dim)


def sent_and_summed(value, axis, dim):
    length = lax.axis_size(axis)
    pieces = lax.all_to_all(cut_along(value, dim, length), axis, 0, 0, tiled=True)
    return jnp.sum(pieces, axis=0)


def replica_terms(wave_row, atten_row, count, source_row, ranges):
    phase = wave_row[:, None] * ranges[None, :]
    magnitude = jnp.exp(-atten_row[:, None] * ranges[None, :]) / jnp.sqrt(phase)
    keep = (jnp.arange(source_row.shape[0], dtype=jnp.int32) < count).astype(jnp.float32)
    hankel_real = magnitude * jnp.cos(phase) * keep[:, None]
    hankel_imag = magnitude * jnp.sin(phase) * keep[:, None]
    coef_real = hankel_real[:, :, None] * source_row[:, None, :]
    coef_imag = hankel_imag[:, :, None] * source_row[:, None, :]
    return (coef_real, coef_imag)


def per_device(cross_spectra, sensor_modes, source_modes, wavenumber, attenuation, mode_counts):
    modes = sensor_modes.shape[1]
    bins_here = sensor_modes.shape[0]
    depth_here = source_modes.shape[2]
    total_bins = bins_here * lax.axis_size("freq")
    whole_spectra = one_exchange(cross_spectra, ("freq", "grid"), ("freq", "grid"), (1, 1), (2, 3))
    whole_modes = lax.all_to_all(sensor_modes, "grid", split_axis=0, concat_axis=2, tiled=True)
    product = jnp.einsum("cbij,bmj->cbim", whole_spectra, whole_modes, precision=HIGH)
    projected = jnp.einsum("bmi,cbin->cbmn", whole_modes, product, precision=HIGH)
    gram = jnp.einsum("bmi,bni->bmn", whole_modes, whole_modes, precision=HIGH)
    stacked_local = jnp.concatenate([projected, gram[None]], 0)
    spectra = collect(stacked_local, "grid", 1)
    count = RANGES // lax.axis_size("freq") * lax.axis_size("freq")
    ranges = 1.0 + jnp.arange(count, dtype=jnp.int32).astype(jnp.float32)

    def one_bin(bin_index, total):
        block = spectra[:, bin_index]
        coupling = jnp.concatenate(
            [jnp.concatenate([block[0], -block[1]], 1), jnp.concatenate([block[1], block[0]], 1)], 0
        )
        coef_real, coef_imag = replica_terms(
            wavenumber[bin_index],
            attenuation[bin_index],
            mode_counts[bin_index],
            source_modes[bin_index],
            ranges,
        )
        coefs = jnp.concatenate([coef_real, coef_imag], 0).reshape(2 * modes, count * depth_here)
        image = jnp.dot(coupling, coefs, precision=HIGH)
        weighted = jnp.einsum(
            "mn,cnx->cmx", block[2], coefs.reshape(2, modes, count * depth_here), precision=HIGH
        )
        weighted = weighted.reshape(2 * modes, count * depth_here)
        numer = jnp.sum(coefs * image, axis=0)
        denom = jnp.sum(coefs * weighted, axis=0)
        return total + (numer / denom).reshape(count, depth_here)

    summed = lax.fori_loop(0, bins_here, one_bin, jnp.zeros((count, depth_here), jnp.float32))
    return sent_and_summed(summed / total_bins, "freq", 0)


def solution(mesh):
    placed = (
        P(None, None, "freq", "grid"),
        P("freq", None, "grid"),
        P("freq", None, "grid"),
        P("freq", None),
        P("freq", None),
        P("freq"),
    )
    return jax.shard_map(
        per_device, mesh=mesh, in_specs=placed, out_specs=P("freq", "grid"), check_vma=False
    )
```

profile of v0, /device:TPU:1, one launch (start us, length us, event | category | flops | bytes accessed | tf_op | source)
XLA Modules:
  0.0 131.5 jit_solution(10738001006194776186)
XLA Ops:
  0.0 0.0 copy-start.1
  0.0 5.8 %all-to-all-start = ((f32[2,96,128]{2,1,0:T(8,128)}), f32[2,96,128]{2,1,0:T(8,128)S(1)}, u32[]{:S(2)}, u32[]{:S(2)}) async-start(f32[2,96,128]{2,1,0:T(8,128)} %param.9), calls=%async_computation | async-start | bytes 196608 | tf_op jit(solution)/shard_map/all_to_all | solution.py:67
  5.8 1.9 %copy.23 = f32[2,64,2,4,128]{4,3,0,2,1:T(4,128)} copy(f32[2,64,2,4,128]{4,3,2,1,0:T(4,128)} %bitcast.129) | data formatting | bytes 1048576 | tf_op jit(solution)/shard_map/reshape | solution.py:14
  7.8 2.7 %all-to-all-done = f32[2,96,128]{2,1,0:T(8,128)S(1)} async-done(((f32[2,96,128]{2,1,0:T(8,128)}), f32[2,96,128]{2,1,0:T(8,128)S(1)}, u32[]{:S(2)}, u32[]{:S(2)}) %all-to-all-start) | async-done | bytes 98336 | tf_op jit(solution)/shard_map/all_to_all | solution.py:67
  10.5 9.1 %all-to-all-start.1 = ((f32[128,2,1,4,128]{4,3,1,2,0:T(4,128)}), f32[128,2,1,4,128]{4,3,1,2,0:T(4,128)S(1)}, u32[]{:S(2)}, u32[]{:S(2)}) async-start(f32[128,2,1,4,128]{4,3,1,2,0:T(4,128)} %bitcast.8), calls=%async_computation.1 | async-start | bytes 1048576 | tf_op jit(solution)/shard_map/all_to_all | solution.py:29
  19.6 0.1 copy.26
  19.7 0.1 reshape.283
  19.8 0.2 convolution_bitcast_fusion.3
  20.0 12.9 %all-to-all-done.1 = f32[128,2,1,4,128]{4,3,1,2,0:T(4,128)S(1)} async-done(((f32[128,2,1,4,128]{4,3,1,2,0:T(4,128)}), f32[128,2,1,4,128]{4,3,1,2,0:T(4,128)S(1)}, u32[]{:S(2)}, u32[]{:S(2)}) %all-to-all-start.1) | async-done | bytes 524320 | tf_op jit(solution)/shard_map/all_to_all | solution.py:29
  32.9 0.1 copy.24
  33.0 0.3 copy.25
  33.4 0.6 convolution_bitcast_fusion.1
  34.0 0.3 convolution_bitcast_fusion.2
  34.3 0.1 copy.28
  34.5 0.7 broadcast_in_dim.25
  35.2 3.4 %all-to-all-start.2 = ((f32[2,3,1,96,96]{4,3,1,2,0:T(8,128)}), f32[2,3,1,96,96]{4,3,1,2,0:T(8,128)S(1)}, u32[]{:S(2)}, u32[]{:S(2)}) async-start(f32[2,3,1,96,96]{4,3,1,2,0:T(8,128)} %broadcast_in_dim.25), calls=%async_computation.2 | async-start | bytes 589824 | tf_op jit(solution)/shard_map/all_to_all | solution.py:36
  38.7 6.3 %all-to-all-done.2 = f32[2,3,1,96,96]{4,3,1,2,0:T(8,128)S(1)} async-done(((f32[2,3,1,96,96]{4,3,1,2,0:T(8,128)}), f32[2,3,1,96,96]{4,3,1,2,0:T(8,128)S(1)}, u32[]{:S(2)}, u32[]{:S(2)}) %all-to-all-start.2) | async-done | bytes 221216 | tf_op jit(solution)/shard_map/all_to_all | solution.py:36
  44.9 0.0 copy-done.2
  44.9 0.0 copy-done.3
  44.9 72.6 %while.15 = (s32[]{:T(128)}, f32[64,128]{1,0:T(8,128)S(1)}, f32[2,96]{1,0:T(2,128)S(1)}, f32[2,96]{1,0:T(2,128)S(1)}, s32[2]{0:T(128)S(1)}, /*index=5*/f32[2,96,...) while((s32[]{:T(128)}, f32[64,128]{1,0:T(8,128)S(1)}, ...), condition=%wide.region_3.0_spmd.clone.clone, body=%wide.region_0.0_spmd.clone.clone.sunk | while | flops 5445426688 | bytes 89226920 | solution.py:98
  45.1 0.6 dynamic_slice.62
  45.7 0.6 compare_convert_fusion.2
  46.3 0.2 fusion.41
  46.5 0.1 copy.44
  46.6 0.1 copy.45
  46.7 1.8 %broadcast_multiply_fusion.4 = (f32[96,64,128]{2,1,0:T(8,128)S(1)}, f32[96,64,128]{2,1,0:T(8,128)S(1)}) fusion(f32[96,64]{1,0:T(8,128)S(1)} %copy.44, f32[96,128]{1,0:T(8,128)S(1)} %dynamic-slice_bitcast_fusion.4, f32[96,64]{1,0:T(8,128)S(1)} %copy.45), kind=kLoop, calls=%fused_computation.9.clone.1 | loop fusion | flops 1572864 | bytes 6389760 | tf_op jit(solution)/shard_map/while/body/eval_jaxpr/mul | solution.py:57
  48.5 2.2 %bitcast_dynamic-update-slice_fusion.4 = f32[192,8192]{1,0:T(8,128)S(1)} fusion(f32[12,8,64,128]{3,2,1,0:T(8,128)S(1)} %bitcast.124), kind=kLoop, calls=%fused_computation.6.clone.1 | loop fusion | bytes 6291456 | tf_op jit(solution)/shard_map/while
  50.7 2.2 %bitcast_dynamic-update-slice_fusion.5 = f32[192,8192]{1,0:T(8,128)S(1)} fusion(f32[192,8192]{1,0:T(8,128)S(1)} %bitcast_dynamic-update-slice_fusion.4, f32[12,8,64,128]{3,2,1,0:T(8,128)S(1)} %bitcast.123), kind=kLoop, calls=%fused_computation.5.clone.1 | loop fusion | bytes 6291456 | tf_op jit(solution)/shard_map/while/body/eval_jaxpr/concatenate | solution.py:88
  53.0 2.6 %copy-done = f32[192,8192]{1,0:T(8,128)} copy-done((f32[192,8192]{1,0:T(8,128)}, f32[192,8192]{1,0:T(8,128)S(1)}, u32[]{:S(2)}) %copy-start) | copy-done | bytes 6291480 | tf_op jit(solution)/shard_map/while
  55.6 6.3 %fusion.43 = f32[8192]{0:T(1024)S(1)} fusion(f32[192,8192]{1,0:T(8,128)S(1)} %bitcast_dynamic-update-slice_fusion.5, f32[96,96]{1,0:T(8,128)S(1)} %get-tuple-element.287, f32[96,96]{1,0:T(8,128)S(1)} %get-tuple-element.288, f32[96,96]{1,0:T(8,128)S(1)} %fusion.42), kind=kOutput, calls=%fused_computation.8.clone.1 | convolution fusion | flops 3627126784 | bytes 6434816 | tf_op jit(solution)/shard_map/while/body/eval_jaxpr/dot_general | solution.py:89
  61.9 3.2 %pad_maximum_fusion.2 = f32[192,64,128]{2,1,0:T(8,128)} fusion(f32[96,64,128]{2,1,0:T(8,128)S(1)} %get-tuple-element.286, f32[96,64,128]{2,1,0:T(8,128)S(1)} %get-tuple-element.285), kind=kLoop, calls=%fused_computation.4.clone.1 | loop fusion | flops 1572864 | bytes 12582912 | tf_op jit(solution)/shard_map/while/body/eval_jaxpr/concatenate | solution.py:88
  65.1 7.2 %reshape.287 = f32[2,96,8192]{2,1,0:T(8,128)} reshape(f32[192,64,128]{2,1,0:T(8,128)} %pad_maximum_fusion.2) | data formatting | bytes 12582912 | tf_op jit(solution)/shard_map/while/body/eval_jaxpr/reshape;while/body/eval_jaxpr/reshape | solution.py:91
  72.3 9.0 %fusion.44 = f32[8192]{0:T(1024)S(1)} fusion(f32[2,96,8192]{2,1,0:T(8,128)} %bitcast.122, f32[2,96,8192]{2,1,0:T(8,128)} %reshape.287, f32[3,1,96,96]{3,2,1,0:T(8,128)S(1)} %dynamic-slice_bitcast_fusion.5), kind=kOutput, calls=%fused_computation.7.clone.1 | convolution fusion | flops 1815076864 | bytes 12664832 | tf_op jit(solution)/shard_map/while/body/eval_jaxpr/mn,cnx->cmx/dot_general | solution.py:90
  81.3 0.6 dynamic_slice.62
  81.9 0.6 compare_convert_fusion.2
  82.5 0.2 fusion.41
  82.7 0.1 copy.44
  82.8 0.1 copy.45
  82.9 1.8 %broadcast_multiply_fusion.4 = (f32[96,64,128]{2,1,0:T(8,128)S(1)}, f32[96,64,128]{2,1,0:T(8,128)S(1)}) fusion(f32[96,64]{1,0:T(8,128)S(1)} %copy.44, f32[96,128]{1,0:T(8,128)S(1)} %dynamic-slice_bitcast_fusion.4, f32[96,64]{1,0:T(8,128)S(1)} %copy.45), kind=kLoop, calls=%fused_computation.9.clone.1 | loop fusion | flops 1572864 | bytes 6389760 | tf_op jit(solution)/shard_map/while/body/eval_jaxpr/mul | solution.py:57
  84.7 2.2 %bitcast_dynamic-update-slice_fusion.4 = f32[192,8192]{1,0:T(8,128)S(1)} fusion(f32[12,8,64,128]{3,2,1,0:T(8,128)S(1)} %bitcast.124), kind=kLoop, calls=%fused_computation.6.clone.1 | loop fusion | bytes 6291456 | tf_op jit(solution)/shard_map/while
  86.9 2.2 %bitcast_dynamic-update-slice_fusion.5 = f32[192,8192]{1,0:T(8,128)S(1)} fusion(f32[192,8192]{1,0:T(8,128)S(1)} %bitcast_dynamic-update-slice_fusion.4, f32[12,8,64,128]{3,2,1,0:T(8,128)S(1)} %bitcast.123), kind=kLoop, calls=%fused_computation.5.clone.1 | loop fusion | bytes 6291456 | tf_op jit(solution)/shard_map/while/body/eval_jaxpr/concatenate | solution.py:88
  89.2 2.6 %copy-done = f32[192,8192]{1,0:T(8,128)} copy-done((f32[192,8192]{1,0:T(8,128)}, f32[192,8192]{1,0:T(8,128)S(1)}, u32[]{:S(2)}) %copy-start) | copy-done | bytes 6291480 | tf_op jit(solution)/shard_map/while
  91.8 6.4 %fusion.43 = f32[8192]{0:T(1024)S(1)} fusion(f32[192,8192]{1,0:T(8,128)S(1)} %bitcast_dynamic-update-slice_fusion.5, f32[96,96]{1,0:T(8,128)S(1)} %get-tuple-element.287, f32[96,96]{1,0:T(8,128)S(1)} %get-tuple-element.288, f32[96,96]{1,0:T(8,128)S(1)} %fusion.42), kind=kOutput, calls=%fused_computation.8.clone.1 | convolution fusion | flops 3627126784 | bytes 6434816 | tf_op jit(solution)/shard_map/while/body/eval_jaxpr/dot_general | solution.py:89
  98.1 3.2 %pad_maximum_fusion.2 = f32[192,64,128]{2,1,0:T(8,128)} fusion(f32[96,64,128]{2,1,0:T(8,128)S(1)} %get-tuple-element.286, f32[96,64,128]{2,1,0:T(8,128)S(1)} %get-tuple-element.285), kind=kLoop, calls=%fused_computation.4.clone.1 | loop fusion | flops 1572864 | bytes 12582912 | tf_op jit(solution)/shard_map/while/body/eval_jaxpr/concatenate | solution.py:88
  101.3 7.2 %reshape.287 = f32[2,96,8192]{2,1,0:T(8,128)} reshape(f32[192,64,128]{2,1,0:T(8,128)} %pad_maximum_fusion.2) | data formatting | bytes 12582912 | tf_op jit(solution)/shard_map/while/body/eval_jaxpr/reshape;while/body/eval_jaxpr/reshape | solution.py:91
  108.5 9.0 %fusion.44 = f32[8192]{0:T(1024)S(1)} fusion(f32[2,96,8192]{2,1,0:T(8,128)} %bitcast.122, f32[2,96,8192]{2,1,0:T(8,128)} %reshape.287, f32[3,1,96,96]{3,2,1,0:T(8,128)S(1)} %dynamic-slice_bitcast_fusion.5), kind=kOutput, calls=%fused_computation.7.clone.1 | convolution fusion | flops 1815076864 | bytes 12664832 | tf_op jit(solution)/shard_map/while/body/eval_jaxpr/mn,cnx->cmx/dot_general | solution.py:90
  117.6 13.4 %all_to_all.30 = f32[64,1,128]{2,1,0:T(1,128)S(1)} all-to-all(f32[64,1,128]{2,1,0:T(1,128)S(1)} %bitcast.130), channel_id=1, replica_groups=mesh['freq'=64,'grid'=2] {'freq'}, dimensions={0} | all-to-all | bytes 65536 | tf_op jit(solution)/shard_map/all_to_all | solution.py:46
  130.9 0.6 reduce_sum.37
  (24 shorter events, 0.2 us)
Async XLA Ops:
  0.0 44.9 %copy-start.2 = (f32[2,96]{1,0:T(2,128)S(1)}, f32[2,96]{1,0:T(2,128)}, u32[]{:S(2)}) copy-start(f32[2,96]{1,0:T(2,128)} %param.12) | copy-start | bytes 2308
  0.0 44.9 %copy-start.3 = (f32[2,96]{1,0:T(2,128)S(1)}, f32[2,96]{1,0:T(2,128)}, u32[]{:S(2)}) copy-start(f32[2,96]{1,0:T(2,128)} %param.11) | copy-start | bytes 2308
  0.0 44.9 %copy-start.4 = (s32[2]{0:T(128)S(1)}, s32[2]{0:T(128)}, u32[]{:S(2)}) copy-start(s32[2]{0:T(128)} %param.13) | copy-start | bytes 28
  0.0 44.9 %copy-start.1 = (f32[2,96,128]{2,1,0:T(8,128)S(1)}, f32[2,96,128]{2,1,0:T(8,128)}, u32[]{:S(2)}) copy-start(f32[2,96,128]{2,1,0:T(8,128)} %param.10) | copy-start | bytes 294916
  0.0 10.5 %all-to-all-start = ((f32[2,96,128]{2,1,0:T(8,128)}), f32[2,96,128]{2,1,0:T(8,128)S(1)}, u32[]{:S(2)}, u32[]{:S(2)}) async-start(f32[2,96,128]{2,1,0:T(8,128)} %param.9), calls=%async_computation | async-start | bytes 196608 | tf_op jit(solution)/shard_map/all_to_all | solution.py:67
  10.5 22.4 %all-to-all-start.1 = ((f32[128,2,1,4,128]{4,3,1,2,0:T(4,128)}), f32[128,2,1,4,128]{4,3,1,2,0:T(4,128)S(1)}, u32[]{:S(2)}, u32[]{:S(2)}) async-start(f32[128,2,1,4,128]{4,3,1,2,0:T(4,128)} %bitcast.8), calls=%async_computation.1 | async-start | bytes 1048576 | tf_op jit(solution)/shard_map/all_to_all | solution.py:29
  35.2 9.7 %all-to-all-start.2 = ((f32[2,3,1,96,96]{4,3,1,2,0:T(8,128)}), f32[2,3,1,96,96]{4,3,1,2,0:T(8,128)S(1)}, u32[]{:S(2)}, u32[]{:S(2)}) async-start(f32[2,3,1,96,96]{4,3,1,2,0:T(8,128)} %broadcast_in_dim.25), calls=%async_computation.2 | async-start | bytes 589824 | tf_op jit(solution)/shard_map/all_to_all | solution.py:36
  52.9 2.7 %copy-start = (f32[192,8192]{1,0:T(8,128)}, f32[192,8192]{1,0:T(8,128)S(1)}, u32[]{:S(2)}) copy-start(f32[192,8192]{1,0:T(8,128)S(1)} %bitcast_dynamic-update-slice_fusion.5) | copy-start | bytes 18874372 | tf_op jit(solution)/shard_map/while
  89.1 2.7 %copy-start = (f32[192,8192]{1,0:T(8,128)}, f32[192,8192]{1,0:T(8,128)S(1)}, u32[]{:S(2)}) copy-start(f32[192,8192]{1,0:T(8,128)S(1)} %bitcast_dynamic-update-slice_fusion.5) | copy-start | bytes 18874372 | tf_op jit(solution)/shard_map/while
where the time goes:
time: 132 us
  local copies, waits for them, and re-layouts  33.2 us (25%)
  matrix products  31.9 us (24%)
  waiting for transfers between devices  21.9 us (17%)
  starting transfers between devices  18.4 us (14%)
  blocking collectives  13.4 us (10%)
  other arithmetic  12.2 us (9%)
    dot_general x2, matrix products, one_bin(): jnp.einsum('mn,cnx->cmx', block[2], coefs.reshape(2, modes, count * depth...  18 us
    reshape x2, local copies, waits for them, and re-layouts, one_bin(): coefs.reshape(2, modes, count * depth_here)  14.3 us
    all_to_all x1, blocking collectives, sent_and_summed(): lax.all_to_all(cut_along(value, dim, length), axis, 0, 0, tiled=True)  13.4 us
    all_to_all x1, waiting for transfers between devices, one_exchange(): lax.all_to_all(pieces, axis, split_axis=0, concat_axis=0, tiled=True)  12.9 us
    dot_general x2, matrix products, one_bin(): image = jnp.dot(coupling, coefs, precision=HIGH)  12.7 us
    while x6, local copies, waits for them, and re-layouts  9.55 us
    all_to_all x1, starting transfers between devices, one_exchange(): lax.all_to_all(pieces, axis, split_axis=0, concat_axis=0, tiled=True)  9.08 us
    concatenate x2, other arithmetic, one_bin(): jnp.concatenate([coef_real, coef_imag], 0)  6.35 us
  transfers between devices with their start and end apart: 3, of which 3 were waited for; matrix products, arithmetic and copies ran while one was open for 2% of the time, Pallas kernels for 0%

commit v1 on v0

v1 whole, which is shorter than its diff:
```python
import jax
import jax.numpy as jnp
from jax import lax
from jax.experimental import pallas as pl
from jax.experimental.pallas import tpu as pltpu
from jax.sharding import PartitionSpec as P

RANGES = 64
LANES = 128
CHUNK = 8

VMEM = pl.BlockSpec(memory_space=pltpu.VMEM)
SMEM = pl.BlockSpec(memory_space=pltpu.SMEM)


def split(value):
    high = value.astype(jnp.bfloat16)
    low = (value - high.astype(jnp.float32)).astype(jnp.bfloat16)
    return high, low


def dot(left, right, contract=((1,), (0,))):
    return lax.dot_general(left, right, (contract, ((), ())), preferred_element_type=jnp.float32)


def pair_kernel(grid_ref, counts_ref, wave_ref, atten_ref, even_ref, odd_ref, row_real, row_imag, col_real, col_imag):
    modes = wave_ref.shape[1]
    mine = grid_ref[0]
    count = counts_ref[mine]
    ranges = 1.0 + lax.broadcasted_iota(jnp.int32, (RANGES, modes), 0).astype(jnp.float32)
    phase = wave_ref[pl.ds(mine, 1), :] * ranges
    magnitude = jnp.exp(-atten_ref[pl.ds(mine, 1), :] * ranges) / jnp.sqrt(phase)
    keep = lax.broadcasted_iota(jnp.int32, (RANGES, modes), 1) < count
    magnitude = jnp.where(keep, magnitude, 0.0)
    for row, col, value in (
        (row_real, col_real, magnitude * jnp.cos(phase)),
        (row_imag, col_imag, magnitude * jnp.sin(phase)),
    ):
        row[...] = jnp.zeros_like(row)
        row[:RANGES, :modes] = value
        col[...] = row[...].T

    def chunk(step, carry):
        base = step * CHUNK
        shift = lax.rem(LANES - base, LANES)
        real = pltpu.roll(col_real[...], shift, 1)
        imag = pltpu.roll(col_imag[...], shift, 1)
        for k in range(CHUNK):
            left_real = jnp.broadcast_to(real[:modes, k : k + 1], (modes, LANES))
            left_imag = jnp.broadcast_to(imag[:modes, k : k + 1], (modes, LANES))
            right_real = row_real[pl.ds(base + k, 1), :]
            right_imag = row_imag[pl.ds(base + k, 1), :]
            even_ref[base + k] = left_real * right_real + left_imag * right_imag
            odd_ref[base + k] = left_real * right_imag - left_imag * right_real
        return carry

    lax.fori_loop(0, RANGES // CHUNK, chunk, 0)


def forms(matrices, weight, tail, sums_ref):
    modes = tail.shape[0]
    depths = tail.shape[1]

    def chunk(step, carry):
        base = step * CHUNK
        left = []
        for k in range(CHUNK):
            high, low = split(matrices(base + k))
            left.append(jnp.concatenate([high, low], 1))
        image = dot(jnp.concatenate(left, 0), weight[...])
        for k in range(CHUNK):
            terms = tail[...] * image[k * modes : (k + 1) * modes]
            sums = jnp.sum(terms.reshape(-1, 8, depths), 0)
            rows = pl.ds(pl.multiple_of((base + k) * 8, 8), 8)
            for half in range(2):
                sums_ref[half, rows, :] = sums[:, half * LANES : (half + 1) * LANES]
        return carry

    lax.fori_loop(0, RANGES // CHUNK, chunk, 0)
    totals = []
    for half in range(2):
        total = sums_ref[half, pl.ds(0, RANGES, stride=8), :]
        for k in range(1, 8):
            total = total + sums_ref[half, pl.ds(k, RANGES, stride=8), :]
        totals.append(total)
    return jnp.concatenate(totals, 1)


def denom_kernel(
    grid_ref, sensor_ref, source_ref, other_ref, even_ref,
    scale_ref, weight_ref, tail_ref, shapes_ref, mixed_ref, whole_ref, sums_ref,
):
    modes = sensor_ref.shape[1]
    mine = grid_ref[0]
    first = mine == 0
    own_shape, other_shape = sensor_ref[mine], other_ref[0]
    own_depth, other_depth = source_ref[mine], other_ref[1]
    whole_ref[...] = jnp.zeros_like(whole_ref)
    whole_ref[:modes, :LANES] = jnp.where(first, own_shape, other_shape)
    whole_ref[:modes, LANES:] = jnp.where(first, other_shape, own_shape)
    shapes = whole_ref[...]
    sensors = shapes.shape[1]
    high, low = split(shapes)
    shapes_ref[:LANES] = high
    shapes_ref[LANES:] = low
    gram = (
        dot(high[:modes], high, ((1,), (1,)))
        + dot(low[:modes], high, ((1,), (1,)))
        + dot(high[:modes], low, ((1,), (1,)))
    )
    source = lax.broadcasted_iota(jnp.int32, (sensors, sensors), 0)
    target = lax.broadcasted_iota(jnp.int32, (sensors, sensors), 1)
    rows = sensors // 4
    order = (source == 4 * (target % rows) + target // rows).astype(jnp.bfloat16)
    mixed_ref[:modes] = dot(high[:modes], order).astype(jnp.bfloat16)
    mixed_ref[modes:] = dot(low[:modes], order).astype(jnp.bfloat16)
    depth = jnp.concatenate(
        [jnp.where(first, own_depth, other_depth), jnp.where(first, other_depth, own_depth)], 1
    )
    depth_high = depth.astype(jnp.bfloat16)
    tail_ref[...] = depth + (depth - depth_high.astype(jnp.float32))
    weight_ref[...] = jnp.zeros_like(weight_ref)
    weight_ref[:modes] = depth_high
    weight_ref[LANES : LANES + modes] = depth_high
    total = forms(lambda j: gram * even_ref[j], weight_ref, tail_ref, sums_ref)
    scale_ref[...] = 1.0 / total


def numer_kernel(
    spectra_ref, scale_ref, weight_ref, tail_ref, shapes_ref, mixed_ref, even_ref, odd_ref,
    power_ref, square_ref, real_ref, imag_ref, sums_ref,
):
    modes = tail_ref.shape[0]
    rows = spectra_ref.shape[0] // 8
    matrix = jnp.concatenate(
        [
            jnp.concatenate([spectra_ref[pl.ds(4 * half + k, rows, stride=8), :] for half in range(2)], 1)
            for k in range(4)
        ],
        0,
    )
    high, low = split(matrix)
    both = dot(mixed_ref[...], high)
    product = both[:modes] + both[modes:] + dot(mixed_ref[:modes], low)
    product_high, product_low = split(product)
    shape_high, shape_low = shapes_ref[:LANES], shapes_ref[LANES:]
    square_ref[...] = jnp.zeros_like(square_ref)
    square_ref[:modes] = (
        dot(product_high, shape_high, ((1,), (1,)))
        + dot(product_low, shape_high, ((1,), (1,)))
        + dot(product_high, shape_low, ((1,), (1,)))
    )
    square = square_ref[...]
    turned = square.T
    real_ref[...] = (0.5 * (square + turned))[:modes]
    imag_ref[...] = (0.5 * (square - turned))[:modes]
    total = forms(
        lambda j: real_ref[...] * even_ref[j] - imag_ref[...] * odd_ref[j], weight_ref, tail_ref, sums_ref
    )
    power = total * scale_ref[...]
    power_ref[pl.ds(0, RANGES, stride=2), :] = power[:, :LANES]
    power_ref[pl.ds(1, RANGES, stride=2), :] = power[:, LANES:]


def shape_of(*shape, dtype=jnp.float32):
    return jax.ShapeDtypeStruct(shape, dtype)


def per_device(cross_spectra, sensor_modes, source_modes, wavenumber, attenuation, mode_counts):
    modes = sensor_modes.shape[1]
    sensors = cross_spectra.shape[3] * 2
    depths = source_modes.shape[2] * 2
    bins = cross_spectra.shape[1]
    mine = lax.axis_index("grid")
    where = mine.reshape(1).astype(jnp.int32)
    other = 1 - mine
    outgoing = jnp.stack(
        [
            lax.dynamic_index_in_dim(sensor_modes, other, 0, False),
            lax.dynamic_index_in_dim(source_modes, other, 0, False),
        ]
    )
    incoming = lax.ppermute(outgoing, "grid", [(0, 1), (1, 0)])
    packed = cross_spectra[0] + cross_spectra[1]
    spectra = lax.all_to_all(packed, ("freq", "grid"), 0, 0, tiled=True)
    even, odd = pl.pallas_call(
        pair_kernel,
        out_shape=[shape_of(RANGES, modes, LANES)] * 2,
        in_specs=[SMEM, SMEM, VMEM, VMEM],
        out_specs=[VMEM] * 2,
        scratch_shapes=[pltpu.VMEM((LANES, LANES), jnp.float32)] * 4,
        cost_estimate=pl.CostEstimate(flops=8_000_000_000, bytes_accessed=0, transcendentals=0),
        name="pairs",
    )(where, mode_counts, wavenumber, attenuation)
    scale, weight, tail, shapes, mixed = pl.pallas_call(
        denom_kernel,
        out_shape=[
            shape_of(RANGES, depths),
            shape_of(2 * LANES, depths, dtype=jnp.bfloat16),
            shape_of(modes, depths),
            shape_of(2 * LANES, sensors, dtype=jnp.bfloat16),
            shape_of(2 * modes, sensors, dtype=jnp.bfloat16),
        ],
        in_specs=[SMEM, VMEM, VMEM, VMEM, VMEM],
        out_specs=[VMEM] * 5,
        scratch_shapes=[pltpu.VMEM((LANES, sensors), jnp.float32), pltpu.VMEM((2, RANGES * 8, LANES), jnp.float32)],
        cost_estimate=pl.CostEstimate(flops=8_000_000_000, bytes_accessed=0, transcendentals=0),
        name="denom",
    )(where, sensor_modes, source_modes, incoming, even)
    power = pl.pallas_call(
        numer_kernel,
        out_shape=shape_of(RANGES * 2, LANES),
        in_specs=[VMEM] * 8,
        out_specs=VMEM,
        scratch_shapes=[
            pltpu.VMEM((LANES, LANES), jnp.float32),
            pltpu.VMEM((modes, LANES), jnp.float32),
            pltpu.VMEM((modes, LANES), jnp.float32),
            pltpu.VMEM((2, RANGES * 8, LANES), jnp.float32),
        ],
        cost_estimate=pl.CostEstimate(flops=8_000_000_000, bytes_accessed=0, transcendentals=0),
        name="numer",
    )(spectra.reshape(-1, LANES), scale, weight, tail, shapes, mixed, even, odd)
    parts = lax.all_to_all(power.reshape(-1, 1, LANES), ("freq", "grid"), 0, 0, tiled=True)
    return jnp.sum(parts.reshape(-1, LANES), 0, keepdims=True) / bins


def solution(mesh):
    placed = (
        P(None, None, "freq", "grid"),
        P("freq", None, "grid"),
        P("freq", None, "grid"),
        P("freq", None),
        P("freq", None),
        P("freq"),
    )
    return jax.shard_map(
        per_device, mesh=mesh, in_specs=placed, out_specs=P("freq", "grid"), check_vma=False
    )
```

time: 132 us -> 55 us (0.42)
  matrix products: 31.9 us -> 0 us
  local copies, waits for them, and re-layouts: 33.2 us -> 2.15 us
  waiting for transfers between devices: 21.9 us -> 0.01 us
  Pallas kernels: 0 us -> 18.3 us
  other arithmetic: 12.2 us -> 2.46 us
  blocking collectives: 13.4 us -> 19.4 us
  starting transfers between devices: 18.4 us -> 12.4 us
    dot_general x7 -> x0, matrix products: 31.9 us -> none  [the longest x2 18 us: one_bin(): jnp.einsum('mn,cnx->cmx', block[2], coefs.reshape(2, modes, count * depth...]
    all_to_all x3 -> x1, waiting for transfers between devices: 21.9 us -> 0.01 us  [per_device(): spectra = lax.all_to_all(packed, ('freq', 'grid'), 0, 0, tiled=True)]
    pallas_call x0 -> x3, Pallas kernels: none -> 18.3 us  [the longest x1 6.6 us: per_device(): pl.pallas_call(numer_kernel, out_shape=shape_of(RANGES * 2, LANES), in_sp...]
    reshape x3 -> x0, local copies, waits for them, and re-layouts: 16.3 us -> none  [the longest x2 14.3 us: one_bin(): coefs.reshape(2, modes, count * depth_here)]
    all_to_all x3 -> x1, starting transfers between devices: 18.3 us -> 7.93 us  [per_device(): spectra = lax.all_to_all(packed, ('freq', 'grid'), 0, 0, tiled=True)]
    while x6 -> x0, local copies, waits for them, and re-layouts: 9.55 us -> none
    concatenate x3 -> x0, other arithmetic: 6.37 us -> none  [the longest x2 6.35 us: one_bin(): jnp.concatenate([coef_real, coef_imag], 0)]
    all_to_all x1, blocking collectives: 13.4 us -> 19.4 us  [per_device(): lax.all_to_all(power.reshape(-1, 1, LANES), ('freq', 'grid'), 0, 0, tiled...]
  transfers between devices with their start and end apart: 3 -> 2, of which waited for: 3 -> 0; matrix products, arithmetic and copies ran while one was open for 2% -> 3% of each run, Pallas kernels for 0% -> 21%
where the time goes in v1:
time: 55 us; the launch traced here: 54.7 us
  blocking collectives  19.4 us (35%)
  Pallas kernels  18.3 us (33%)
  starting transfers between devices  12.4 us (23%)
  other arithmetic  2.46 us (4%)
  local copies, waits for them, and re-layouts  2.15 us (4%)
    all_to_all x1, blocking collectives, per_device(): lax.all_to_all(power.reshape(-1, 1, LANES), ('freq', 'grid'), 0, 0, tiled...  19.4 us
    all_to_all x1, starting transfers between devices, per_device(): spectra = lax.all_to_all(packed, ('freq', 'grid'), 0, 0, tiled=True)  7.93 us
    pallas_call x1, Pallas kernels, per_device(): pl.pallas_call(numer_kernel, out_shape=shape_of(RANGES * 2, LANES), in_sp...  6.6 us
    pallas_call x1, Pallas kernels, per_device(): pl.pallas_call(pair_kernel, out_shape=[shape_of(RANGES, modes, LANES)] *...  6.46 us
    pallas_call x1, Pallas kernels, per_device(): pl.pallas_call(denom_kernel, out_shape=[shape_of(RANGES, depths), shape_o...  5.21 us
    ppermute x1, starting transfers between devices, per_device(): incoming = lax.ppermute(outgoing, 'grid', [(0, 1), (1, 0)])  4.49 us
    add x1, other arithmetic, per_device(): packed = cross_spectra[0] + cross_spectra[1]  1.79 us
    unnamed x4, local copies, waits for them, and re-layouts  1.32 us
  transfers between devices with their start and end apart: 2, of which 0 were waited for; matrix products, arithmetic and copies ran while one was open for 3% of the time, Pallas kernels for 21%

profile of v1, /device:TPU:1, one launch (start us, length us, event | category | flops | bytes accessed | tf_op | source)
XLA Modules:
  0.0 54.7 jit_solution(12007299630954518607)
XLA Ops:
  0.0 0.8 %constant_dynamic-slice_fusion = (f32[1,96,128]{2,1,0:T(8,128)S(1)}, f32[1,96,128]{2,1,0:T(8,128)S(1)}) fusion(f32[2,96,128]{2,1,0:T(8,128)} %source_ref.1, s32[]{:T(128)S(6)} %select_n.5, f32[2,96,128]{2,1,0:T(8,128)} %sensor_ref.1), kind=kLoop, calls=%fused_computation.3 | loop fusion | bytes 196612 | tf_op jit(solution)/shard_map/jit(dynamic_index_in_dim)/dynamic_slice | solution.py:180
  0.8 4.5 %collective-permute-start = (f32[2,96,128]{2,1,0:T(8,128)S(1)}, f32[2,96,128]{2,1,0:T(8,128)S(1)}, u32[]{:S(2)}, u32[]{:S(2)}) collective-permute-start(f32[2,96,128]{2,1,0:T(8,128)S(1)} %pad_maximum_fusion), channel_id=1, source_target_pairs={{0,1},{1,0},{2,3},{3,2},{4,5},{5,4},{6,7},{7,6},{8,9},{9,8},{10,11... | collective-permute-start | bytes 294920 | tf_op jit(solution)/shard_map/ppermute | solution.py:183
  5.3 1.8 %add_bitcast_fusion = f32[128,4,128]{2,1,0:T(4,128)} fusion(f32[2,128,4,128]{3,2,1,0:T(4,128)} %param.6), kind=kLoop, calls=%fused_computation | loop fusion | flops 65536 | bytes 786432 | tf_op jit(solution)/shard_map/add | solution.py:184
  7.1 7.9 %all-to-all-start = ((f32[128,4,128]{2,1,0:T(4,128)}), f32[128,4,128]{2,1,0:T(4,128)S(1)}, u32[]{:S(2)}, u32[]{:S(2)}) async-start(f32[128,4,128]{2,1,0:T(4,128)} %add_bitcast_fusion), calls=%async_computation | async-start | bytes 524288 | tf_op jit(solution)/shard_map/all_to_all | solution.py:185
  15.1 6.5 %pairs.1 = (f32[64,96,128]{2,1,0:T(8,128)}, f32[64,96,128]{2,1,0:T(8,128)}) custom-call(s32[1]{0:T(128)} %bitcast.2.grid_ref, s32[2]{0:T(128)} %counts_ref.1, f32[2,96]{1,0:T(2,128)} %wave_ref.1, f32[2,96]{1,0:T(2,128)} %atten_ref.1), custom_call_target="tpu_custom_call" | custom-call | flops 8000000000 | tf_op jit(solution)/shard_map/pairs/pallas_call | solution.py:186
  21.5 0.0 collective-permute-done.other_ref
  21.5 0.0 copy-start.1
  21.5 0.6 %copy-done.1 = f32[2,96,128]{2,1,0:T(8,128)} copy-done((f32[2,96,128]{2,1,0:T(8,128)}, f32[2,96,128]{2,1,0:T(8,128)S(1)}, u32[]{:S(2)}) %copy-start.1) | copy-done | bytes 98328
  22.1 5.2 %denom.1 = (f32[64,256]{1,0:T(8,128)}, bf16[256,256]{1,0:T(8,128)(2,1)}, f32[96,256]{1,0:T(8,128)}, bf16[256,256]{1,0:T(8,128)(2,1)}, bf16[192,256]{1,0:T(8,128)(2,1)}) custom-call(s32[1]{0:T(128)} %bitcast.2.grid_ref, f32[2,96,128]{2,1,0:T(8,128)} %sensor_ref.1, f32[2,96,128]{2,1,0:T(8,128)} %source_ref.1, f32[2,96,128]{2,1,0:T(8,128)} %copy-done.1, ...), custom_call_target="tpu_custom_call" | custom-call | flops 8000000000 | tf_op jit(solution)/shard_map/denom/pallas_call | solution.py:195
  27.4 0.0 all-to-all-done
  27.4 0.0 copy-start
  27.4 0.7 %copy-done = f32[128,4,128]{2,1,0:T(4,128)} copy-done((f32[128,4,128]{2,1,0:T(4,128)}, f32[128,4,128]{2,1,0:T(4,128)S(1)}, u32[]{:S(2)}) %copy-start) | copy-done | bytes 262168
  28.1 6.6 %numer.1 = f32[128,128]{1,0:T(8,128)} custom-call(f32[512,128]{1,0:T(8,128)} %bitcast.9, f32[64,256]{1,0:T(8,128)} %get-tuple-element.13.scale_ref, bf16[256,256]{1,0:T(8,128)(2,1)} %get-tuple-element.14.weight_ref, f32[96,256]{1,0:T(8,128)} %get-tuple-element.15.tail_ref, bf16[256,256]{1,0:T(8,128)(2,1)} %get-tuple-element.16.shapes_ref, ...), custom_call_target="tpu_custom_call" | custom-call | flops 8000000000 | tf_op jit(solution)/shard_map/numer/pallas_call | solution.py:210
  34.7 19.4 %all_to_all.10 = f32[128,1,128]{2,1,0:T(1,128)S(1)} all-to-all(f32[128,1,128]{2,1,0:T(1,128)} %bitcast.10), channel_id=1, replica_groups=mesh['freq'=64,'grid'=2] {'freq','grid'}, dimensions={0} | all-to-all | bytes 131072 | tf_op jit(solution)/shard_map/all_to_all | solution.py:224
  54.0 0.2 reduce_sum.9
  54.2 0.5 multiply_bitcast_fusion
  (1 shorter events, 0.0 us)
Async XLA Ops:
  0.8 20.7 %collective-permute-start = (f32[2,96,128]{2,1,0:T(8,128)S(1)}, f32[2,96,128]{2,1,0:T(8,128)S(1)}, u32[]{:S(2)}, u32[]{:S(2)}) collective-permute-start(f32[2,96,128]{2,1,0:T(8,128)S(1)} %pad_maximum_fusion), channel_id=1, source_target_pairs={{0,1},{1,0},{2,3},{3,2},{4,5},{5,4},{6,7},{7,6},{8,9},{9,8},{10,11... | collective-permute-start | bytes 294920 | tf_op jit(solution)/shard_map/ppermute | solution.py:183
  7.1 20.2 %all-to-all-start = ((f32[128,4,128]{2,1,0:T(4,128)}), f32[128,4,128]{2,1,0:T(4,128)S(1)}, u32[]{:S(2)}, u32[]{:S(2)}) async-start(f32[128,4,128]{2,1,0:T(4,128)} %add_bitcast_fusion), calls=%async_computation | async-start | bytes 524288 | tf_op jit(solution)/shard_map/all_to_all | solution.py:185
  21.5 0.6 %copy-start.1 = (f32[2,96,128]{2,1,0:T(8,128)}, f32[2,96,128]{2,1,0:T(8,128)S(1)}, u32[]{:S(2)}) copy-start(f32[2,96,128]{2,1,0:T(8,128)S(1)} %collective-permute-done.other_ref) | copy-start | bytes 294916
  27.4 0.7 %copy-start = (f32[128,4,128]{2,1,0:T(4,128)}, f32[128,4,128]{2,1,0:T(4,128)S(1)}, u32[]{:S(2)}) copy-start(f32[128,4,128]{2,1,0:T(4,128)S(1)} %all-to-all-done) | copy-start | bytes 786436

commit v2 on v1

v2 whole, which is shorter than its diff:
```python
import functools

import jax
import jax.numpy as jnp
from jax import lax
from jax.experimental import pallas as pl
from jax.experimental.pallas import tpu as pltpu
from jax.sharding import PartitionSpec as P

RANGES = 64
LANES = 128
CHUNK = 32
CHUNKS = RANGES // CHUNK

VMEM = pl.BlockSpec(memory_space=pltpu.VMEM)
SMEM = pl.BlockSpec(memory_space=pltpu.SMEM)
COST = pl.CostEstimate(flops=8_000_000_000, bytes_accessed=0, transcendentals=0)
PARAMS = pltpu.CompilerParams(vmem_limit_bytes=8 * 1024 * 1024)


def split(value):
    high = value.astype(jnp.bfloat16)
    low = (value - high.astype(jnp.float32)).astype(jnp.bfloat16)
    return high, low


def dot(left, right, contract=((1,), (0,))):
    return lax.dot_general(left, right, (contract, ((), ())), preferred_element_type=jnp.float32)


def pack_kernel(grid_ref, spectra_ref, sensor_ref, source_ref, packed_ref, outgoing_ref):
    packed_ref[...] = spectra_ref[0] + spectra_ref[1]
    outgoing_ref[0] = sensor_ref[0]
    outgoing_ref[1] = source_ref[0]


def forms(matrices, weight, tail, sums_ref):
    modes = tail.shape[0]
    depths = tail.shape[1]

    def chunk(step, carry):
        base = step * CHUNK
        left = []
        for k in range(CHUNK):
            high, low = split(matrices(step, k))
            left.append(jnp.concatenate([high, low], 1))
        image = dot(jnp.concatenate(left, 0), weight[...])
        for k in range(CHUNK):
            terms = tail[...] * image[k * modes : (k + 1) * modes]
            sums = jnp.sum(terms.reshape(-1, 8, depths), 0)
            rows = pl.ds(pl.multiple_of((base + k) * 8, 8), 8)
            for half in range(2):
                sums_ref[half, rows, :] = sums[:, half * LANES : (half + 1) * LANES]
        return carry

    lax.fori_loop(0, CHUNKS, chunk, 0)
    totals = []
    for half in range(2):
        total = sums_ref[half, pl.ds(0, RANGES, stride=8), :]
        for k in range(1, 8):
            total = total + sums_ref[half, pl.ds(k, RANGES, stride=8), :]
        totals.append(total)
    return jnp.concatenate(totals, 1)


def pair(rows_ref, cols_ref, step, k):
    modes = cols_ref.shape[2]
    at = pl.ds(step * CHUNK + k, 1)
    left = [jnp.broadcast_to(cols_ref[part, step, :, k : k + 1], (modes, LANES)) for part in range(2)]
    right = [rows_ref[part, at, :] for part in range(2)]
    return left, right


def denom_kernel(
    bins, grid_ref, counts_ref, wave_ref, atten_ref, sensor_ref, source_ref, other_ref,
    scale_ref, weight_ref, tail_ref, shapes_ref, mixed_ref, rows_ref, cols_ref, whole_ref, sums_ref,
):
    modes = sensor_ref.shape[1]
    mine = grid_ref[0]
    first = mine == 0
    count = counts_ref[mine]

    ranges = 1.0 + lax.broadcasted_iota(jnp.int32, (RANGES, modes), 0).astype(jnp.float32)
    phase = wave_ref[pl.ds(mine, 1), :] * ranges
    magnitude = jnp.exp(-atten_ref[pl.ds(mine, 1), :] * ranges) / jnp.sqrt(phase)
    keep = lax.broadcasted_iota(jnp.int32, (RANGES, modes), 1) < count
    magnitude = jnp.where(keep, magnitude, 0.0)
    rows_ref[...] = jnp.zeros_like(rows_ref)
    for part, value in enumerate((magnitude * jnp.cos(phase), magnitude * jnp.sin(phase))):
        rows_ref[part, :RANGES, :modes] = value
        turned = rows_ref[part].T
        for step in range(CHUNKS):
            moved = pltpu.roll(turned, LANES - CHUNK * step, 1) if step else turned
            cols_ref[part, step] = moved[:modes]

    own_shape, other_shape = sensor_ref[mine], other_ref[0]
    own_depth, other_depth = source_ref[mine], other_ref[1]
    whole_ref[...] = jnp.zeros_like(whole_ref)
    whole_ref[:modes, :LANES] = jnp.where(first, own_shape, other_shape)
    whole_ref[:modes, LANES:] = jnp.where(first, other_shape, own_shape)
    shapes = whole_ref[...]
    sensors = shapes.shape[1]
    high, low = split(shapes)
    shapes_ref[:LANES] = high
    shapes_ref[LANES:] = low
    gram = (
        dot(high[:modes], high, ((1,), (1,)))
        + dot(low[:modes], high, ((1,), (1,)))
        + dot(high[:modes], low, ((1,), (1,)))
    )
    source = lax.broadcasted_iota(jnp.int32, (sensors, sensors), 0)
    target = lax.broadcasted_iota(jnp.int32, (sensors, sensors), 1)
    rows = sensors // 4
    order = (source == 4 * (target % rows) + target // rows).astype(jnp.bfloat16)
    mixed_ref[:modes] = dot(high[:modes], order).astype(jnp.bfloat16)
    mixed_ref[modes:] = dot(low[:modes], order).astype(jnp.bfloat16)
    depth = jnp.concatenate(
        [jnp.where(first, own_depth, other_depth), jnp.where(first, other_depth, own_depth)], 1
    )
    depth_high = depth.astype(jnp.bfloat16)
    tail_ref[...] = depth + (depth - depth_high.astype(jnp.float32))
    weight_ref[...] = jnp.zeros_like(weight_ref)
    weight_ref[:modes] = depth_high
    weight_ref[LANES : LANES + modes] = depth_high

    def matrices(step, k):
        (left_real, left_imag), (right_real, right_imag) = pair(rows_ref, cols_ref, step, k)
        return gram * (left_real * right_real + left_imag * right_imag)

    total = forms(matrices, weight_ref, tail_ref, sums_ref)
    scale_ref[...] = 1.0 / (total * bins)


def numer_kernel(
    spectra_ref, scale_ref, weight_ref, tail_ref, shapes_ref, mixed_ref, rows_ref, cols_ref,
    power_ref, square_ref, real_ref, imag_ref, sums_ref,
):
    modes = tail_ref.shape[0]
    rows = spectra_ref.shape[0] // 8
    matrix = jnp.concatenate(
        [
            jnp.concatenate([spectra_ref[pl.ds(4 * half + k, rows, stride=8), :] for half in range(2)], 1)
            for k in range(4)
        ],
        0,
    )
    high, low = split(matrix)
    both = dot(mixed_ref[...], high)
    product = both[:modes] + both[modes:] + dot(mixed_ref[:modes], low)
    product_high, product_low = split(product)
    shape_high, shape_low = shapes_ref[:LANES], shapes_ref[LANES:]
    square_ref[...] = jnp.zeros_like(square_ref)
    square_ref[:modes] = (
        dot(product_high, shape_high, ((1,), (1,)))
        + dot(product_low, shape_high, ((1,), (1,)))
        + dot(product_high, shape_low, ((1,), (1,)))
    )
    square = square_ref[...]
    turned = square.T
    real_ref[...] = (0.5 * (square + turned))[:modes]
    imag_ref[...] = (0.5 * (square - turned))[:modes]

    def matrices(step, k):
        (left_real, left_imag), (right_real, right_imag) = pair(rows_ref, cols_ref, step, k)
        even = left_real * right_real + left_imag * right_imag
        odd = left_real * right_imag - left_imag * right_real
        return real_ref[...] * even - imag_ref[...] * odd

    power = forms(matrices, weight_ref, tail_ref, sums_ref) * scale_ref[...]
    power_ref[pl.ds(0, RANGES, stride=2), :] = power[:, :LANES]
    power_ref[pl.ds(1, RANGES, stride=2), :] = power[:, LANES:]


def shape_of(*shape, dtype=jnp.float32):
    return jax.ShapeDtypeStruct(shape, dtype)


def per_device(cross_spectra, sensor_modes, source_modes, wavenumber, attenuation, mode_counts):
    modes = sensor_modes.shape[1]
    sensors = cross_spectra.shape[3] * 2
    depths = source_modes.shape[2] * 2
    bins = cross_spectra.shape[1]
    mine = lax.axis_index("grid").astype(jnp.int32)
    where = mine.reshape(1)
    steps = 4
    block = bins * 4 // steps
    packed, outgoing = pl.pallas_call(
        pack_kernel,
        grid_spec=pltpu.PrefetchScalarGridSpec(
            num_scalar_prefetch=1,
            grid=(steps,),
            in_specs=[
                pl.BlockSpec((2, block, LANES), lambda i, at: (0, i, 0)),
                pl.BlockSpec((1, modes, LANES), lambda i, at: (1 - at[0], 0, 0)),
                pl.BlockSpec((1, modes, LANES), lambda i, at: (1 - at[0], 0, 0)),
            ],
            out_specs=[
                pl.BlockSpec((block, LANES), lambda i, at: (i, 0)),
                pl.BlockSpec((2, modes, LANES), lambda i, at: (0, 0, 0)),
            ],
        ),
        out_shape=[shape_of(bins * 4, LANES), shape_of(2, modes, LANES)],
        name="pack",
    )(where, cross_spectra.reshape(2, bins * 4, LANES), sensor_modes, source_modes)
    incoming = lax.ppermute(outgoing, "grid", [(0, 1), (1, 0)])
    spectra = lax.all_to_all(packed.reshape(bins, 4, LANES), ("freq", "grid"), 0, 0, tiled=True)
    tables = pl.pallas_call(
        functools.partial(denom_kernel, bins),
        out_shape=[
            shape_of(RANGES, depths),
            shape_of(2 * LANES, depths, dtype=jnp.bfloat16),
            shape_of(modes, depths),
            shape_of(2 * LANES, sensors, dtype=jnp.bfloat16),
            shape_of(2 * modes, sensors, dtype=jnp.bfloat16),
            shape_of(2, LANES, LANES),
            shape_of(2, CHUNKS, modes, LANES),
        ],
        in_specs=[SMEM, SMEM, VMEM, VMEM, VMEM, VMEM, VMEM],
        out_specs=[VMEM] * 7,
        scratch_shapes=[
            pltpu.VMEM((LANES, sensors), jnp.float32),
            pltpu.VMEM((2, RANGES * 8, LANES), jnp.float32),
        ],
        cost_estimate=COST,
        compiler_params=PARAMS,
        name="denom",
    )(where, mode_counts, wavenumber, attenuation, sensor_modes, source_modes, incoming)
    power = pl.pallas_call(
        numer_kernel,
        out_shape=shape_of(RANGES * 2, LANES),
        in_specs=[VMEM] * 8,
        out_specs=VMEM,
        scratch_shapes=[
            pltpu.VMEM((LANES, LANES), jnp.float32),
            pltpu.VMEM((modes, LANES), jnp.float32),
            pltpu.VMEM((modes, LANES), jnp.float32),
            pltpu.VMEM((2, RANGES * 8, LANES), jnp.float32),
        ],
        cost_estimate=COST,
        compiler_params=PARAMS,
        name="numer",
    )(spectra.reshape(-1, LANES), *tables)
    parts = lax.all_to_all(power.reshape(-1, 1, LANES), ("freq", "grid"), 0, 0, tiled=True)
    return jnp.sum(parts.reshape(-1, LANES), 0, keepdims=True)


def solution(mesh):
    placed = (
        P(None, None, "freq", "grid"),
        P("freq", None, "grid"),
        P("freq", None, "grid"),
        P("freq", None),
        P("freq", None),
        P("freq"),
    )
    return jax.shard_map(
        per_device, mesh=mesh, in_specs=placed, out_specs=P("freq", "grid"), check_vma=False
    )
```

time: 55 us -> 43.8 us (0.80)
  Pallas kernels: 18.3 us -> 9.02 us
  waiting for transfers between devices: 0.01 us -> 7.73 us
  blocking collectives: 19.4 us -> 13.7 us
  local copies, waits for them, and re-layouts: 2.15 us -> 0.02 us
  other arithmetic: 2.46 us -> 0.66 us
    all_to_all x1, waiting for transfers between devices: 0.01 us -> 7.73 us  [per_device(): lax.all_to_all(packed.reshape(bins, 4, LANES), ('freq', 'grid'), 0, 0, ti...]
    all_to_all x1, blocking collectives: 19.4 us -> 13.7 us  [per_device(): lax.all_to_all(power.reshape(-1, 1, LANES), ('freq', 'grid'), 0, 0, tiled...]
    pallas_call x2, Pallas kernels: 11.7 us -> 6.3 us  [the longest x1 3.18 us: per_device(): pl.pallas_call(functools.partial(denom_kernel, bins), out_shape=[shape_of...]
    pallas_call x1, Pallas kernels: 6.6 us -> 2.72 us  [per_device(): pl.pallas_call(numer_kernel, out_shape=shape_of(RANGES * 2, LANES), in_sp...]
    add x1 -> x0, other arithmetic: 1.79 us -> none  [per_device(): packed = cross_spectra[0] + cross_spectra[1]]
    unnamed x4 -> x10, local copies, waits for them, and re-layouts: 1.32 us -> 0.02 us
    dynamic_slice x1 -> x0, local copies, waits for them, and re-layouts: 0.83 us -> none  [per_device(): lax.dynamic_index_in_dim(source_modes, other, 0, False)]
  transfers between devices with their start and end apart: 2 -> 2, of which waited for: 0 -> 1; matrix products, arithmetic and copies ran while one was open for 3% -> 0% of each run, Pallas kernels for 21% -> 7%
where the time goes in v2:
time: 43.8 us; the launch traced here: 43.5 us
  blocking collectives  13.7 us (31%)
  starting transfers between devices  12.3 us (28%)
  Pallas kernels  9.02 us (21%)
  waiting for transfers between devices  7.73 us (18%)
  other arithmetic  0.66 us (2%)
    all_to_all x1, blocking collectives, per_device(): lax.all_to_all(power.reshape(-1, 1, LANES), ('freq', 'grid'), 0, 0, tiled...  13.7 us
    all_to_all x1, starting transfers between devices, per_device(): lax.all_to_all(packed.reshape(bins, 4, LANES), ('freq', 'grid'), 0, 0, ti...  7.93 us
    all_to_all x1, waiting for transfers between devices, per_device(): lax.all_to_all(packed.reshape(bins, 4, LANES), ('freq', 'grid'), 0, 0, ti...  7.73 us
    ppermute x1, starting transfers between devices, per_device(): incoming = lax.ppermute(outgoing, 'grid', [(0, 1), (1, 0)])  4.41 us
    pallas_call x1, Pallas kernels, per_device(): pl.pallas_call(functools.partial(denom_kernel, bins), out_shape=[shape_of...  3.18 us
    pallas_call x1, Pallas kernels, per_device(): pl.pallas_call(pack_kernel, grid_spec=pltpu.PrefetchScalarGridSpec(num_sc...  3.12 us
    pallas_call x1, Pallas kernels, per_device(): pl.pallas_call(numer_kernel, out_shape=shape_of(RANGES * 2, LANES), in_sp...  2.72 us
  transfers between devices with their start and end apart: 2, of which 1 were waited for; matrix products, arithmetic and copies ran while one was open for 0% of the time, Pallas kernels for 7%

profile of v2, /device:TPU:1, one launch (start us, length us, event | category | flops | bytes accessed | tf_op | source)
XLA Modules:
  0.0 43.5 jit_solution(378076986214017490)
XLA Ops:
  0.0 3.1 %pack.1 = (f32[512,128]{1,0:T(8,128)}, f32[2,96,128]{2,1,0:T(8,128)}) custom-call(s32[1]{0:T(128)} %bitcast.grid_ref, f32[2,512,128]{2,1,0:T(8,128)} %bitcast.10, f32[2,96,128]{2,1,0:T(8,128)} %sensor_ref.3, f32[2,96,128]{2,1,0:T(8,128)} %source_ref.3), custom_call_target="tpu_custom_call" | custom-call | tf_op jit(solution)/shard_map/pack/pallas_call | solution.py:187
  3.1 4.4 %collective-permute-start = (f32[2,96,128]{2,1,0:T(8,128)}, f32[2,96,128]{2,1,0:T(8,128)S(1)}, u32[]{:S(2)}, u32[]{:S(2)}) collective-permute-start(f32[2,96,128]{2,1,0:T(8,128)} %get-tuple-element.15), channel_id=1, source_target_pairs={{0,1},{1,0},{2,3},{3,2},{4,5},{5,4},{6,7},{7,6},{8,9},{9,8},{10,11... | collective-permute-start | bytes 294920 | tf_op jit(solution)/shard_map/ppermute | solution.py:205
  7.5 0.0 copy-start
  7.5 0.0 copy-start.1
  7.5 0.0 copy-start.2
  7.5 0.0 copy-start.3
  7.5 0.0 copy-start.4
  7.6 7.9 %all-to-all-start = ((f32[128,4,128]{2,1,0:T(4,128)}), f32[128,4,128]{2,1,0:T(4,128)S(1)}, u32[]{:S(2)}, u32[]{:S(2)}) async-start(f32[128,4,128]{2,1,0:T(4,128)} %bitcast.11), calls=%async_computation | async-start | bytes 524288 | tf_op jit(solution)/shard_map/all_to_all | solution.py:206
  15.5 0.0 collective-permute-done.other_ref
  15.5 0.0 copy-done
  15.5 0.0 copy-done.1
  15.5 0.0 copy-done.2
  15.5 0.0 copy-done.3
  15.6 0.0 copy-done.4
  15.6 3.2 %denom.1 = (f32[64,256]{1,0:T(8,128)S(1)}, bf16[256,256]{1,0:T(8,128)(2,1)S(1)}, f32[96,256]{1,0:T(8,128)S(1)}, bf16[256,256]{1,0:T(8,128)(2,1)S(1)}, bf16[192,2...) custom-call(s32[1]{0:T(128)} %bitcast.grid_ref, s32[2]{0:T(128)S(1)} %copy-done.4, ...), custom_call_target="tpu_custom_call" | custom-call | flops 8000000000 | tf_op jit(solution)/shard_map/denom/pallas_call | solution.py:207
  18.7 7.7 %all-to-all-done = f32[128,4,128]{2,1,0:T(4,128)S(1)} async-done(((f32[128,4,128]{2,1,0:T(4,128)}), f32[128,4,128]{2,1,0:T(4,128)S(1)}, u32[]{:S(2)}, u32[]{:S(2)}) %all-to-all-start) | async-done | bytes 262176 | tf_op jit(solution)/shard_map/all_to_all | solution.py:206
  26.5 2.7 %numer.1 = f32[128,128]{1,0:T(8,128)S(1)} custom-call(f32[512,128]{1,0:T(8,128)S(1)} %bitcast.8, f32[64,256]{1,0:T(8,128)S(1)} %get-tuple-element.16.scale_ref, bf16[256,256]{1,0:T(8,128)(2,1)S(1)} %get-tuple-element.17.weight_ref, f32[96,256]{1,0:T(8,128)S(1)} %get-tuple-element.18.tail_ref, bf16[256,256]{1,0:T(8,128)(2,1)S(1)} %get-tuple-element.19.shapes_ref, ...), custom_call_target="tpu_custom_call" | custom-call | flops 8000000000 | tf_op jit(solution)/shard_map/numer/pallas_call | solution.py:228
  29.2 13.7 %all_to_all.10 = f32[128,1,128]{2,1,0:T(1,128)S(1)} all-to-all(f32[128,1,128]{2,1,0:T(1,128)S(1)} %bitcast.9), channel_id=1, replica_groups=mesh['freq'=64,'grid'=2] {'freq','grid'}, dimensions={0} | all-to-all | bytes 131072 | tf_op jit(solution)/shard_map/all_to_all | solution.py:243
  42.9 0.7 %reduce_sum.9 = f32[128]{0:T(128)} reduce(f32[128,1,128]{2,1,0:T(1,128)S(1)} %all_to_all.10, f32[]{:T(128)} %constant.1.clone.1), dimensions={0,1}, to_apply=%region_0.0 | reduce | flops 16256 | bytes 66052 | tf_op jit(solution)/shard_map/reduce_sum | solution.py:244
Async XLA Ops:
  3.1 12.4 %collective-permute-start = (f32[2,96,128]{2,1,0:T(8,128)}, f32[2,96,128]{2,1,0:T(8,128)S(1)}, u32[]{:S(2)}, u32[]{:S(2)}) collective-permute-start(f32[2,96,128]{2,1,0:T(8,128)} %get-tuple-element.15), channel_id=1, source_target_pairs={{0,1},{1,0},{2,3},{3,2},{4,5},{5,4},{6,7},{7,6},{8,9},{9,8},{10,11... | collective-permute-start | bytes 294920 | tf_op jit(solution)/shard_map/ppermute | solution.py:205
  7.5 8.0 %copy-start = (f32[2,96,128]{2,1,0:T(8,128)S(1)}, f32[2,96,128]{2,1,0:T(8,128)}, u32[]{:S(2)}) copy-start(f32[2,96,128]{2,1,0:T(8,128)} %sensor_ref.3) | copy-start | bytes 294916
  7.5 8.0 %copy-start.1 = (f32[2,96,128]{2,1,0:T(8,128)S(1)}, f32[2,96,128]{2,1,0:T(8,128)}, u32[]{:S(2)}) copy-start(f32[2,96,128]{2,1,0:T(8,128)} %source_ref.3) | copy-start | bytes 294916
  7.5 8.0 %copy-start.2 = (f32[2,96]{1,0:T(2,128)S(1)}, f32[2,96]{1,0:T(2,128)}, u32[]{:S(2)}) copy-start(f32[2,96]{1,0:T(2,128)} %wave_ref.1) | copy-start | bytes 2308
  7.5 8.0 %copy-start.3 = (f32[2,96]{1,0:T(2,128)S(1)}, f32[2,96]{1,0:T(2,128)}, u32[]{:S(2)}) copy-start(f32[2,96]{1,0:T(2,128)} %atten_ref.1) | copy-start | bytes 2308
  7.5 8.0 %copy-start.4 = (s32[2]{0:T(128)S(1)}, s32[2]{0:T(128)}, u32[]{:S(2)}) copy-start(s32[2]{0:T(128)} %counts_ref.1) | copy-start | bytes 28
  7.6 18.9 %all-to-all-start = ((f32[128,4,128]{2,1,0:T(4,128)}), f32[128,4,128]{2,1,0:T(4,128)S(1)}, u32[]{:S(2)}, u32[]{:S(2)}) async-start(f32[128,4,128]{2,1,0:T(4,128)} %bitcast.11), calls=%async_computation | async-start | bytes 524288 | tf_op jit(solution)/shard_map/all_to_all | solution.py:206

commit v3 on v2

--- a/solution.py
+++ b/solution.py
@@ -10,9 +10,11 @@
 RANGES = 64
 LANES = 128
 CHUNK = 32
+PIECES = 2
 CHUNKS = RANGES // CHUNK
 
 VMEM = pl.BlockSpec(memory_space=pltpu.VMEM)
+ANY = pl.BlockSpec(memory_space=pl.ANY)
 SMEM = pl.BlockSpec(memory_space=pltpu.SMEM)
 COST = pl.CostEstimate(flops=8_000_000_000, bytes_accessed=0, transcendentals=0)
 PARAMS = pltpu.CompilerParams(vmem_limit_bytes=8 * 1024 * 1024)
@@ -28,10 +30,33 @@
     return lax.dot_general(left, right, (contract, ((), ())), preferred_element_type=jnp.float32)
 
 
-def pack_kernel(grid_ref, spectra_ref, sensor_ref, source_ref, packed_ref, outgoing_ref):
-    packed_ref[...] = spectra_ref[0] + spectra_ref[1]
-    outgoing_ref[0] = sensor_ref[0]
-    outgoing_ref[1] = source_ref[0]
+def pack_kernel(
+    grid_ref, spectra_ref, sensor_ref, source_ref, packed_ref, outgoing_ref, both_ref, sum_ref, half_ref, in_sem, out_sem
+):
+    other = 1 - grid_ref[0]
+    rows = packed_ref.shape[0] // PIECES
+    halves = [
+        pltpu.make_async_copy(ref.at[other], half_ref.at[k], in_sem.at[PIECES + k])
+        for k, ref in enumerate((sensor_ref, source_ref))
+    ]
+    pieces = [
+        pltpu.make_async_copy(spectra_ref.at[:, pl.ds(k * rows, rows)], both_ref.at[k], in_sem.at[k])
+        for k in range(PIECES)
+    ]
+    for copy in halves + pieces:
+        copy.start()
+    sends = []
+    for k, copy in enumerate(halves):
+        copy.wait()
+        sends.append(pltpu.make_async_copy(half_ref.at[k], outgoing_ref.at[k], out_sem.at[PIECES + k]))
+        sends[-1].start()
+    for k, copy in enumerate(pieces):
+        copy.wait()
+        sum_ref[k] = both_ref[k, 0] + both_ref[k, 1]
+        sends.append(pltpu.make_async_copy(sum_ref.at[k], packed_ref.at[pl.ds(k * rows, rows)], out_sem.at[k]))
+        sends[-1].start()
+    for copy in sends:
+        copy.wait()
 
 
 def forms(matrices, weight, tail, sums_ref):
@@ -182,24 +207,19 @@
     bins = cross_spectra.shape[1]
     mine = lax.axis_index("grid").astype(jnp.int32)
     where = mine.reshape(1)
-    steps = 4
-    block = bins * 4 // steps
+    rows = bins * 4 // PIECES
     packed, outgoing = pl.pallas_call(
         pack_kernel,
-        grid_spec=pltpu.PrefetchScalarGridSpec(
-            num_scalar_prefetch=1,
-            grid=(steps,),
-            in_specs=[
-                pl.BlockSpec((2, block, LANES), lambda i, at: (0, i, 0)),
-                pl.BlockSpec((1, modes, LANES), lambda i, at: (1 - at[0], 0, 0)),
-                pl.BlockSpec((1, modes, LANES), lambda i, at: (1 - at[0], 0, 0)),
-            ],
-            out_specs=[
-                pl.BlockSpec((block, LANES), lambda i, at: (i, 0)),
-                pl.BlockSpec((2, modes, LANES), lambda i, at: (0, 0, 0)),
-            ],
-        ),
         out_shape=[shape_of(bins * 4, LANES), shape_of(2, modes, LANES)],
+        in_specs=[SMEM, ANY, ANY, ANY],
+        out_specs=[ANY] * 2,
+        scratch_shapes=[
+            pltpu.VMEM((PIECES, 2, rows, LANES), jnp.float32),
+            pltpu.VMEM((PIECES, rows, LANES), jnp.float32),
+            pltpu.VMEM((2, modes, LANES), jnp.float32),
+            pltpu.SemaphoreType.DMA((PIECES + 2,)),
+            pltpu.SemaphoreType.DMA((PIECES + 2,)),
+        ],
         name="pack",
     )(where, cross_spectra.reshape(2, bins * 4, LANES), sensor_modes, source_modes)
     incoming = lax.ppermute(outgoing, "grid", [(0, 1), (1, 0)])
@@ -217,10 +237,7 @@
         ],
         in_specs=[SMEM, SMEM, VMEM, VMEM, VMEM, VMEM, VMEM],
         out_specs=[VMEM] * 7,
-        scratch_shapes=[
-            pltpu.VMEM((LANES, sensors), jnp.float32),
-            pltpu.VMEM((2, RANGES * 8, LANES), jnp.float32),
-        ],
+        scratch_shapes=[pltpu.VMEM((LANES, sensors), jnp.float32), pltpu.VMEM((2, RANGES * 8, LANES), jnp.float32)],
         cost_estimate=COST,
         compiler_params=PARAMS,
         name="denom",

time: 43.8 us -> 42.5 us (0.970)
  Pallas kernels: 9.02 us -> 7.72 us
    pallas_call x1, Pallas kernels: 3.12 us -> 1.83 us  [per_device(): pl.pallas_call(pack_kernel, out_shape=[shape_of(bins * 4, LANES), shape_o...]
  transfers between devices with their start and end apart: 2 -> 2, of which waited for: 1 -> 1; matrix products, arithmetic and copies ran while one was open for 0% -> 0% of each run, Pallas kernels for 7% -> 8%
where the time goes in v3:
time: 42.5 us; the launch traced here: 42.3 us
  blocking collectives  13.7 us (32%)
  starting transfers between devices  12.4 us (29%)
  waiting for transfers between devices  7.73 us (18%)
  Pallas kernels  7.72 us (18%)
  other arithmetic  0.66 us (2%)
    all_to_all x1, blocking collectives, per_device(): lax.all_to_all(power.reshape(-1, 1, LANES), ('freq', 'grid'), 0, 0, tiled...  13.7 us
    all_to_all x1, starting transfers between devices, per_device(): lax.all_to_all(packed.reshape(bins, 4, LANES), ('freq', 'grid'), 0, 0, ti...  7.93 us
    all_to_all x1, waiting for transfers between devices, per_device(): lax.all_to_all(packed.reshape(bins, 4, LANES), ('freq', 'grid'), 0, 0, ti...  7.73 us
    ppermute x1, starting transfers between devices, per_device(): incoming = lax.ppermute(outgoing, 'grid', [(0, 1), (1, 0)])  4.49 us
    pallas_call x1, Pallas kernels, per_device(): pl.pallas_call(functools.partial(denom_kernel, bins), out_shape=[shape_of...  3.18 us
    pallas_call x1, Pallas kernels, per_device(): pl.pallas_call(numer_kernel, out_shape=shape_of(RANGES * 2, LANES), in_sp...  2.72 us
    pallas_call x1, Pallas kernels, per_device(): pl.pallas_call(pack_kernel, out_shape=[shape_of(bins * 4, LANES), shape_o...  1.83 us
  transfers between devices with their start and end apart: 2, of which 1 were waited for; matrix products, arithmetic and copies ran while one was open for 0% of the time, Pallas kernels for 8%

profile of v3, /device:TPU:1, one launch (start us, length us, event | category | flops | bytes accessed | tf_op | source)
XLA Modules:
  0.0 42.3 jit_solution(14850236024618199467)
XLA Ops:
  0.0 1.8 %pack.1 = (f32[512,128]{1,0:T(8,128)}, f32[2,96,128]{2,1,0:T(8,128)}) custom-call(s32[1]{0:T(128)} %bitcast.grid_ref, f32[2,512,128]{2,1,0:T(8,128)} %bitcast.10, f32[2,96,128]{2,1,0:T(8,128)} %sensor_ref.3, f32[2,96,128]{2,1,0:T(8,128)} %source_ref.3), custom_call_target="tpu_custom_call" | custom-call | tf_op jit(solution)/shard_map/pack/pallas_call | solution.py:211
  1.8 4.5 %collective-permute-start = (f32[2,96,128]{2,1,0:T(8,128)}, f32[2,96,128]{2,1,0:T(8,128)S(1)}, u32[]{:S(2)}, u32[]{:S(2)}) collective-permute-start(f32[2,96,128]{2,1,0:T(8,128)} %get-tuple-element.15), channel_id=1, source_target_pairs={{0,1},{1,0},{2,3},{3,2},{4,5},{5,4},{6,7},{7,6},{8,9},{9,8},{10,11... | collective-permute-start | bytes 294920 | tf_op jit(solution)/shard_map/ppermute | solution.py:225
  6.3 0.0 copy-start
  6.3 0.0 copy-start.1
  6.3 0.0 copy-start.2
  6.3 0.0 copy-start.3
  6.3 0.0 copy-start.4
  6.4 7.9 %all-to-all-start = ((f32[128,4,128]{2,1,0:T(4,128)}), f32[128,4,128]{2,1,0:T(4,128)S(1)}, u32[]{:S(2)}, u32[]{:S(2)}) async-start(f32[128,4,128]{2,1,0:T(4,128)} %bitcast.11), calls=%async_computation | async-start | bytes 524288 | tf_op jit(solution)/shard_map/all_to_all | solution.py:226
  14.3 0.0 collective-permute-done.other_ref
  14.3 0.0 copy-done
  14.3 0.0 copy-done.1
  14.3 0.0 copy-done.2
  14.3 0.0 copy-done.3
  14.3 0.0 copy-done.4
  14.4 3.2 %denom.1 = (f32[64,256]{1,0:T(8,128)S(1)}, bf16[256,256]{1,0:T(8,128)(2,1)S(1)}, f32[96,256]{1,0:T(8,128)S(1)}, bf16[256,256]{1,0:T(8,128)(2,1)S(1)}, bf16[192,2...) custom-call(s32[1]{0:T(128)} %bitcast.grid_ref, s32[2]{0:T(128)S(1)} %copy-done.4, ...), custom_call_target="tpu_custom_call" | custom-call | flops 8000000000 | tf_op jit(solution)/shard_map/denom/pallas_call | solution.py:227
  17.5 7.7 %all-to-all-done = f32[128,4,128]{2,1,0:T(4,128)S(1)} async-done(((f32[128,4,128]{2,1,0:T(4,128)}), f32[128,4,128]{2,1,0:T(4,128)S(1)}, u32[]{:S(2)}, u32[]{:S(2)}) %all-to-all-start) | async-done | bytes 262176 | tf_op jit(solution)/shard_map/all_to_all | solution.py:226
  25.3 2.7 %numer.1 = f32[128,128]{1,0:T(8,128)S(1)} custom-call(f32[512,128]{1,0:T(8,128)S(1)} %bitcast.8, f32[64,256]{1,0:T(8,128)S(1)} %get-tuple-element.16.scale_ref, bf16[256,256]{1,0:T(8,128)(2,1)S(1)} %get-tuple-element.17.weight_ref, f32[96,256]{1,0:T(8,128)S(1)} %get-tuple-element.18.tail_ref, bf16[256,256]{1,0:T(8,128)(2,1)S(1)} %get-tuple-element.19.shapes_ref, ...), custom_call_target="tpu_custom_call" | custom-call | flops 8000000000 | tf_op jit(solution)/shard_map/numer/pallas_call | solution.py:245
  28.0 13.7 %all_to_all.10 = f32[128,1,128]{2,1,0:T(1,128)S(1)} all-to-all(f32[128,1,128]{2,1,0:T(1,128)S(1)} %bitcast.9), channel_id=1, replica_groups=mesh['freq'=64,'grid'=2] {'freq','grid'}, dimensions={0} | all-to-all | bytes 131072 | tf_op jit(solution)/shard_map/all_to_all | solution.py:260
  41.7 0.7 %reduce_sum.9 = f32[128]{0:T(128)} reduce(f32[128,1,128]{2,1,0:T(1,128)S(1)} %all_to_all.10, f32[]{:T(128)} %constant.1.clone.1), dimensions={0,1}, to_apply=%region_0.0 | reduce | flops 16256 | bytes 66052 | tf_op jit(solution)/shard_map/reduce_sum | solution.py:261
Async XLA Ops:
  1.8 12.5 %collective-permute-start = (f32[2,96,128]{2,1,0:T(8,128)}, f32[2,96,128]{2,1,0:T(8,128)S(1)}, u32[]{:S(2)}, u32[]{:S(2)}) collective-permute-start(f32[2,96,128]{2,1,0:T(8,128)} %get-tuple-element.15), channel_id=1, source_target_pairs={{0,1},{1,0},{2,3},{3,2},{4,5},{5,4},{6,7},{7,6},{8,9},{9,8},{10,11... | collective-permute-start | bytes 294920 | tf_op jit(solution)/shard_map/ppermute | solution.py:225
  6.3 8.0 %copy-start = (f32[2,96,128]{2,1,0:T(8,128)S(1)}, f32[2,96,128]{2,1,0:T(8,128)}, u32[]{:S(2)}) copy-start(f32[2,96,128]{2,1,0:T(8,128)} %sensor_ref.3) | copy-start | bytes 294916
  6.3 8.0 %copy-start.1 = (f32[2,96,128]{2,1,0:T(8,128)S(1)}, f32[2,96,128]{2,1,0:T(8,128)}, u32[]{:S(2)}) copy-start(f32[2,96,128]{2,1,0:T(8,128)} %source_ref.3) | copy-start | bytes 294916
  6.3 8.0 %copy-start.2 = (f32[2,96]{1,0:T(2,128)S(1)}, f32[2,96]{1,0:T(2,128)}, u32[]{:S(2)}) copy-start(f32[2,96]{1,0:T(2,128)} %wave_ref.1) | copy-start | bytes 2308
  6.3 8.0 %copy-start.3 = (f32[2,96]{1,0:T(2,128)S(1)}, f32[2,96]{1,0:T(2,128)}, u32[]{:S(2)}) copy-start(f32[2,96]{1,0:T(2,128)} %atten_ref.1) | copy-start | bytes 2308
  6.3 8.0 %copy-start.4 = (s32[2]{0:T(128)S(1)}, s32[2]{0:T(128)}, u32[]{:S(2)}) copy-start(s32[2]{0:T(128)} %counts_ref.1) | copy-start | bytes 28
  6.4 18.9 %all-to-all-start = ((f32[128,4,128]{2,1,0:T(4,128)}), f32[128,4,128]{2,1,0:T(4,128)S(1)}, u32[]{:S(2)}, u32[]{:S(2)}) async-start(f32[128,4,128]{2,1,0:T(4,128)} %bitcast.11), calls=%async_computation | async-start | bytes 524288 | tf_op jit(solution)/shard_map/all_to_all | solution.py:226

commit v4 on v3

--- a/solution.py
+++ b/solution.py
@@ -9,9 +9,8 @@
 
 RANGES = 64
 LANES = 128
-CHUNK = 32
+CHUNK = 16
 PIECES = 2
-CHUNKS = RANGES // CHUNK
 
 VMEM = pl.BlockSpec(memory_space=pltpu.VMEM)
 ANY = pl.BlockSpec(memory_space=pl.ANY)
@@ -59,26 +58,27 @@
         copy.wait()
 
 
-def forms(matrices, weight, tail, sums_ref):
+def forms(exact, twice_ref, square_ref, weight, tail, sums_ref):
     modes = tail.shape[0]
     depths = tail.shape[1]
-
-    def chunk(step, carry):
-        base = step * CHUNK
+    for base in range(0, RANGES, CHUNK):
         left = []
-        for k in range(CHUNK):
-            high, low = split(matrices(step, k))
+        before = now = None
+        for j in range(base, base + CHUNK):
+            if j < base + 2:
+                later = exact(j)
+            else:
+                later = twice_ref[...] * now - square_ref[...] * before
+            before, now = now, later
+            high, low = split(now)
             left.append(jnp.concatenate([high, low], 1))
         image = dot(jnp.concatenate(left, 0), weight[...])
         for k in range(CHUNK):
             terms = tail[...] * image[k * modes : (k + 1) * modes]
             sums = jnp.sum(terms.reshape(-1, 8, depths), 0)
-            rows = pl.ds(pl.multiple_of((base + k) * 8, 8), 8)
+            row = (base + k) * 8
             for half in range(2):
-                sums_ref[half, rows, :] = sums[:, half * LANES : (half + 1) * LANES]
-        return carry
-
-    lax.fori_loop(0, CHUNKS, chunk, 0)
+                sums_ref[half, row : row + 8, :] = sums[:, half * LANES : (half + 1) * LANES]
     totals = []
     for half in range(2):
         total = sums_ref[half, pl.ds(0, RANGES, stride=8), :]
@@ -88,35 +88,40 @@
     return jnp.concatenate(totals, 1)
 
 
-def pair(rows_ref, cols_ref, step, k):
-    modes = cols_ref.shape[2]
-    at = pl.ds(step * CHUNK + k, 1)
-    left = [jnp.broadcast_to(cols_ref[part, step, :, k : k + 1], (modes, LANES)) for part in range(2)]
-    right = [rows_ref[part, at, :] for part in range(2)]
+def pair(rows_ref, cols_ref, j):
+    modes = cols_ref.shape[1]
+    left = [jnp.broadcast_to(cols_ref[part, :, j : j + 1], (modes, LANES)) for part in range(2)]
+    right = [rows_ref[part, j : j + 1, :] for part in range(2)]
     return left, right
 
 
 def denom_kernel(
     bins, grid_ref, counts_ref, wave_ref, atten_ref, sensor_ref, source_ref, other_ref,
-    scale_ref, weight_ref, tail_ref, shapes_ref, mixed_ref, rows_ref, cols_ref, whole_ref, sums_ref,
+    scale_ref, weight_ref, tail_ref, shapes_ref, mixed_ref, rows_ref, cols_ref, twice_ref, square_ref,
+    whole_ref, spread_ref, sums_ref,
 ):
     modes = sensor_ref.shape[1]
     mine = grid_ref[0]
     first = mine == 0
     count = counts_ref[mine]
 
+    wave = wave_ref[pl.ds(mine, 1), :]
+    atten = atten_ref[pl.ds(mine, 1), :]
     ranges = 1.0 + lax.broadcasted_iota(jnp.int32, (RANGES, modes), 0).astype(jnp.float32)
-    phase = wave_ref[pl.ds(mine, 1), :] * ranges
-    magnitude = jnp.exp(-atten_ref[pl.ds(mine, 1), :] * ranges) / jnp.sqrt(phase)
+    phase = wave * ranges
     keep = lax.broadcasted_iota(jnp.int32, (RANGES, modes), 1) < count
-    magnitude = jnp.where(keep, magnitude, 0.0)
+    magnitude = jnp.where(keep, jnp.exp(-atten * ranges) / jnp.sqrt(wave), 0.0)
     rows_ref[...] = jnp.zeros_like(rows_ref)
     for part, value in enumerate((magnitude * jnp.cos(phase), magnitude * jnp.sin(phase))):
         rows_ref[part, :RANGES, :modes] = value
-        turned = rows_ref[part].T
-        for step in range(CHUNKS):
-            moved = pltpu.roll(turned, LANES - CHUNK * step, 1) if step else turned
-            cols_ref[part, step] = moved[:modes]
+        cols_ref[part] = rows_ref[part].T[:modes]
+    spread_ref[...] = jnp.zeros_like(spread_ref)
+    spread_ref[0, :, :modes] = jnp.broadcast_to(wave, (LANES, modes))
+    spread_ref[1, :, :modes] = jnp.broadcast_to(atten, (LANES, modes))
+    waves, attens = spread_ref[0], spread_ref[1]
+    decay = jnp.exp(-(attens.T + attens))
+    twice_ref[...] = (2.0 * decay * jnp.cos(waves - waves.T))[:modes]
+    square_ref[...] = (decay * decay)[:modes]
 
     own_shape, other_shape = sensor_ref[mine], other_ref[0]
     own_depth, other_depth = source_ref[mine], other_ref[1]
@@ -148,17 +153,17 @@
     weight_ref[:modes] = depth_high
     weight_ref[LANES : LANES + modes] = depth_high
 
-    def matrices(step, k):
-        (left_real, left_imag), (right_real, right_imag) = pair(rows_ref, cols_ref, step, k)
+    def exact(j):
+        (left_real, left_imag), (right_real, right_imag) = pair(rows_ref, cols_ref, j)
         return gram * (left_real * right_real + left_imag * right_imag)
 
-    total = forms(matrices, weight_ref, tail_ref, sums_ref)
+    total = forms(exact, twice_ref, square_ref, weight_ref, tail_ref, sums_ref)
     scale_ref[...] = 1.0 / (total * bins)
 
 
 def numer_kernel(
-    spectra_ref, scale_ref, weight_ref, tail_ref, shapes_ref, mixed_ref, rows_ref, cols_ref,
-    power_ref, square_ref, real_ref, imag_ref, sums_ref,
+    spectra_ref, scale_ref, weight_ref, tail_ref, shapes_ref, mixed_ref, rows_ref, cols_ref, twice_ref, square_ref,
+    power_ref, whole_ref, real_ref, imag_ref, sums_ref,
 ):
     modes = tail_ref.shape[0]
     rows = spectra_ref.shape[0] // 8
@@ -174,24 +179,24 @@
     product = both[:modes] + both[modes:] + dot(mixed_ref[:modes], low)
     product_high, product_low = split(product)
     shape_high, shape_low = shapes_ref[:LANES], shapes_ref[LANES:]
-    square_ref[...] = jnp.zeros_like(square_ref)
-    square_ref[:modes] = (
+    whole_ref[...] = jnp.zeros_like(whole_ref)
+    whole_ref[:modes] = (
         dot(product_high, shape_high, ((1,), (1,)))
         + dot(product_low, shape_high, ((1,), (1,)))
         + dot(product_high, shape_low, ((1,), (1,)))
     )
-    square = square_ref[...]
+    square = whole_ref[...]
     turned = square.T
     real_ref[...] = (0.5 * (square + turned))[:modes]
     imag_ref[...] = (0.5 * (square - turned))[:modes]
 
-    def matrices(step, k):
-        (left_real, left_imag), (right_real, right_imag) = pair(rows_ref, cols_ref, step, k)
+    def exact(j):
+        (left_real, left_imag), (right_real, right_imag) = pair(rows_ref, cols_ref, j)
         even = left_real * right_real + left_imag * right_imag
         odd = left_real * right_imag - left_imag * right_real
         return real_ref[...] * even - imag_ref[...] * odd
 
-    power = forms(matrices, weight_ref, tail_ref, sums_ref) * scale_ref[...]
+    power = forms(exact, twice_ref, square_ref, weight_ref, tail_ref, sums_ref) * scale_ref[...]
     power_ref[pl.ds(0, RANGES, stride=2), :] = power[:, :LANES]
     power_ref[pl.ds(1, RANGES, stride=2), :] = power[:, LANES:]
 
@@ -233,11 +238,17 @@
             shape_of(2 * LANES, sensors, dtype=jnp.bfloat16),
             shape_of(2 * modes, sensors, dtype=jnp.bfloat16),
             shape_of(2, LANES, LANES),
-            shape_of(2, CHUNKS, modes, LANES),
+            shape_of(2, modes, LANES),
+            shape_of(modes, LANES),
+            shape_of(modes, LANES),
         ],
         in_specs=[SMEM, SMEM, VMEM, VMEM, VMEM, VMEM, VMEM],
-        out_specs=[VMEM] * 7,
-        scratch_shapes=[pltpu.VMEM((LANES, sensors), jnp.float32), pltpu.VMEM((2, RANGES * 8, LANES), jnp.float32)],
+        out_specs=[VMEM] * 9,
+        scratch_shapes=[
+            pltpu.VMEM((LANES, sensors), jnp.float32),
+            pltpu.VMEM((2, LANES, LANES), jnp.float32),
+            pltpu.VMEM((2, RANGES * 8, LANES), jnp.float32),
+        ],
         cost_estimate=COST,
         compiler_params=PARAMS,
         name="denom",
@@ -245,7 +256,7 @@
     power = pl.pallas_call(
         numer_kernel,
         out_shape=shape_of(RANGES * 2, LANES),
-        in_specs=[VMEM] * 8,
+        in_specs=[VMEM] * 10,
         out_specs=VMEM,
         scratch_shapes=[
             pltpu.VMEM((LANES, LANES), jnp.float32),

time: 42.5 us -> 41.6 us (0.979)
  Pallas kernels: 7.72 us -> 5.98 us
  waiting for transfers between devices: 7.73 us -> 8.53 us
    pallas_call x1, Pallas kernels: 2.72 us -> 1.77 us  [per_device(): pl.pallas_call(numer_kernel, out_shape=shape_of(RANGES * 2, LANES), in_sp...]
    pallas_call x1, Pallas kernels: 3.18 us -> 2.38 us  [per_device(): pl.pallas_call(functools.partial(denom_kernel, bins), out_shape=[shape_of...]
    all_to_all x1, waiting for transfers between devices: 7.73 us -> 8.53 us  [per_device(): lax.all_to_all(packed.reshape(bins, 4, LANES), ('freq', 'grid'), 0, 0, ti...]
  transfers between devices with their start and end apart: 2 -> 2, of which waited for: 1 -> 1; matrix products, arithmetic and copies ran while one was open for 0% -> 0% of each run, Pallas kernels for 8% -> 6%
where the time goes in v4:
time: 41.6 us; the launch traced here: 41.4 us
  blocking collectives  13.7 us (33%)
  starting transfers between devices  12.4 us (30%)
  waiting for transfers between devices  8.53 us (21%)
  Pallas kernels  5.98 us (14%)
  other arithmetic  0.66 us (2%)
    all_to_all x1, blocking collectives, per_device(): lax.all_to_all(power.reshape(-1, 1, LANES), ('freq', 'grid'), 0, 0, tiled...  13.7 us
    all_to_all x1, waiting for transfers between devices, per_device(): lax.all_to_all(packed.reshape(bins, 4, LANES), ('freq', 'grid'), 0, 0, ti...  8.53 us
    all_to_all x1, starting transfers between devices, per_device(): lax.all_to_all(packed.reshape(bins, 4, LANES), ('freq', 'grid'), 0, 0, ti...  7.93 us
    ppermute x1, starting transfers between devices, per_device(): incoming = lax.ppermute(outgoing, 'grid', [(0, 1), (1, 0)])  4.49 us
    pallas_call x1, Pallas kernels, per_device(): pl.pallas_call(functools.partial(denom_kernel, bins), out_shape=[shape_of...  2.38 us
    pallas_call x1, Pallas kernels, per_device(): pl.pallas_call(pack_kernel, out_shape=[shape_of(bins * 4, LANES), shape_o...  1.83 us
    pallas_call x1, Pallas kernels, per_device(): pl.pallas_call(numer_kernel, out_shape=shape_of(RANGES * 2, LANES), in_sp...  1.77 us
  transfers between devices with their start and end apart: 2, of which 1 were waited for; matrix products, arithmetic and copies ran while one was open for 0% of the time, Pallas kernels for 6%

profile of v4, /device:TPU:1, one launch (start us, length us, event | category | flops | bytes accessed | tf_op | source)
XLA Modules:
  0.0 41.4 jit_solution(9653558005001000279)
XLA Ops:
  0.0 1.8 %pack.1 = (f32[512,128]{1,0:T(8,128)}, f32[2,96,128]{2,1,0:T(8,128)}) custom-call(s32[1]{0:T(128)} %bitcast.grid_ref, f32[2,512,128]{2,1,0:T(8,128)} %bitcast.10, f32[2,96,128]{2,1,0:T(8,128)} %sensor_ref.3, f32[2,96,128]{2,1,0:T(8,128)} %source_ref.3), custom_call_target="tpu_custom_call" | custom-call | tf_op jit(solution)/shard_map/pack/pallas_call | solution.py:216
  1.8 4.5 %collective-permute-start = (f32[2,96,128]{2,1,0:T(8,128)}, f32[2,96,128]{2,1,0:T(8,128)S(1)}, u32[]{:S(2)}, u32[]{:S(2)}) collective-permute-start(f32[2,96,128]{2,1,0:T(8,128)} %get-tuple-element.17), channel_id=1, source_target_pairs={{0,1},{1,0},{2,3},{3,2},{4,5},{5,4},{6,7},{7,6},{8,9},{9,8},{10,11... | collective-permute-start | bytes 294920 | tf_op jit(solution)/shard_map/ppermute | solution.py:230
  6.3 0.0 copy-start
  6.3 0.0 copy-start.1
  6.3 0.0 copy-start.2
  6.3 0.0 copy-start.3
  6.3 0.0 copy-start.4
  6.4 7.9 %all-to-all-start = ((f32[128,4,128]{2,1,0:T(4,128)}), f32[128,4,128]{2,1,0:T(4,128)S(1)}, u32[]{:S(2)}, u32[]{:S(2)}) async-start(f32[128,4,128]{2,1,0:T(4,128)} %bitcast.11), calls=%async_computation | async-start | bytes 524288 | tf_op jit(solution)/shard_map/all_to_all | solution.py:231
  14.3 0.0 collective-permute-done.other_ref
  14.3 0.0 copy-done
  14.3 0.0 copy-done.1
  14.3 0.0 copy-done.2
  14.3 0.0 copy-done.3
  14.3 0.0 copy-done.4
  14.4 2.4 %denom.1 = (f32[64,256]{1,0:T(8,128)S(1)}, bf16[256,256]{1,0:T(8,128)(2,1)S(1)}, f32[96,256]{1,0:T(8,128)S(1)}, bf16[256,256]{1,0:T(8,128)(2,1)S(1)}, bf16[192,2...) custom-call(s32[1]{0:T(128)} %bitcast.grid_ref, ...), custom_call_target="tpu_custom_call" | custom-call | flops 8000000000 | tf_op jit(solution)/shard_map/denom/pallas_call | solution.py:232
  16.7 8.5 %all-to-all-done = f32[128,4,128]{2,1,0:T(4,128)S(1)} async-done(((f32[128,4,128]{2,1,0:T(4,128)}), f32[128,4,128]{2,1,0:T(4,128)S(1)}, u32[]{:S(2)}, u32[]{:S(2)}) %all-to-all-start) | async-done | bytes 262176 | tf_op jit(solution)/shard_map/all_to_all | solution.py:231
  25.3 1.8 %numer.1 = f32[128,128]{1,0:T(8,128)S(1)} custom-call(f32[512,128]{1,0:T(8,128)S(1)} %bitcast.8, f32[64,256]{1,0:T(8,128)S(1)} %get-tuple-element.18.scale_ref, bf16[256,256]{1,0:T(8,128)(2,1)S(1)} %get-tuple-element.19.weight_ref, f32[96,256]{1,0:T(8,128)S(1)} %get-tuple-element.20.tail_ref, bf16[256,256]{1,0:T(8,128)(2,1)S(1)} %get-tuple-element.21.shapes_ref, ...), custom_call_target="tpu_custom_call" | custom-call | flops 8000000000 | tf_op jit(solution)/shard_map/numer/pallas_call | solution.py:256
  27.1 13.7 %all_to_all.10 = f32[128,1,128]{2,1,0:T(1,128)S(1)} all-to-all(f32[128,1,128]{2,1,0:T(1,128)S(1)} %bitcast.9), channel_id=1, replica_groups=mesh['freq'=64,'grid'=2] {'freq','grid'}, dimensions={0} | all-to-all | bytes 131072 | tf_op jit(solution)/shard_map/all_to_all | solution.py:271
  40.7 0.7 %reduce_sum.9 = f32[128]{0:T(128)} reduce(f32[128,1,128]{2,1,0:T(1,128)S(1)} %all_to_all.10, f32[]{:T(128)} %constant.1.clone.1), dimensions={0,1}, to_apply=%region_0.0 | reduce | flops 16256 | bytes 66052 | tf_op jit(solution)/shard_map/reduce_sum | solution.py:272
Async XLA Ops:
  1.8 12.5 %collective-permute-start = (f32[2,96,128]{2,1,0:T(8,128)}, f32[2,96,128]{2,1,0:T(8,128)S(1)}, u32[]{:S(2)}, u32[]{:S(2)}) collective-permute-start(f32[2,96,128]{2,1,0:T(8,128)} %get-tuple-element.17), channel_id=1, source_target_pairs={{0,1},{1,0},{2,3},{3,2},{4,5},{5,4},{6,7},{7,6},{8,9},{9,8},{10,11... | collective-permute-start | bytes 294920 | tf_op jit(solution)/shard_map/ppermute | solution.py:230
  6.3 8.0 %copy-start = (f32[2,96,128]{2,1,0:T(8,128)S(1)}, f32[2,96,128]{2,1,0:T(8,128)}, u32[]{:S(2)}) copy-start(f32[2,96,128]{2,1,0:T(8,128)} %sensor_ref.3) | copy-start | bytes 294916
  6.3 8.0 %copy-start.1 = (f32[2,96,128]{2,1,0:T(8,128)S(1)}, f32[2,96,128]{2,1,0:T(8,128)}, u32[]{:S(2)}) copy-start(f32[2,96,128]{2,1,0:T(8,128)} %source_ref.3) | copy-start | bytes 294916
  6.3 8.0 %copy-start.2 = (f32[2,96]{1,0:T(2,128)S(1)}, f32[2,96]{1,0:T(2,128)}, u32[]{:S(2)}) copy-start(f32[2,96]{1,0:T(2,128)} %wave_ref.1) | copy-start | bytes 2308
  6.3 8.0 %copy-start.3 = (f32[2,96]{1,0:T(2,128)S(1)}, f32[2,96]{1,0:T(2,128)}, u32[]{:S(2)}) copy-start(f32[2,96]{1,0:T(2,128)} %atten_ref.1) | copy-start | bytes 2308
  6.3 8.0 %copy-start.4 = (s32[2]{0:T(128)S(1)}, s32[2]{0:T(128)}, u32[]{:S(2)}) copy-start(s32[2]{0:T(128)} %counts_ref.1) | copy-start | bytes 28
  6.4 18.9 %all-to-all-start = ((f32[128,4,128]{2,1,0:T(4,128)}), f32[128,4,128]{2,1,0:T(4,128)S(1)}, u32[]{:S(2)}, u32[]{:S(2)}) async-start(f32[128,4,128]{2,1,0:T(4,128)} %bitcast.11), calls=%async_computation | async-start | bytes 524288 | tf_op jit(solution)/shard_map/all_to_all | solution.py:231

commit v5 on v4

--- a/solution.py
+++ b/solution.py
@@ -7,13 +7,13 @@
 from jax.experimental.pallas import tpu as pltpu
 from jax.sharding import PartitionSpec as P
 
+
 RANGES = 64
 LANES = 128
-CHUNK = 16
-PIECES = 2
+CHUNK = 32
 
 VMEM = pl.BlockSpec(memory_space=pltpu.VMEM)
-ANY = pl.BlockSpec(memory_space=pl.ANY)
+HBM = pl.BlockSpec(memory_space=pltpu.HBM)
 SMEM = pl.BlockSpec(memory_space=pltpu.SMEM)
 COST = pl.CostEstimate(flops=8_000_000_000, bytes_accessed=0, transcendentals=0)
 PARAMS = pltpu.CompilerParams(vmem_limit_bytes=8 * 1024 * 1024)
@@ -29,33 +29,20 @@
     return lax.dot_general(left, right, (contract, ((), ())), preferred_element_type=jnp.float32)
 
 
-def pack_kernel(
-    grid_ref, spectra_ref, sensor_ref, source_ref, packed_ref, outgoing_ref, both_ref, sum_ref, half_ref, in_sem, out_sem
-):
-    other = 1 - grid_ref[0]
-    rows = packed_ref.shape[0] // PIECES
-    halves = [
-        pltpu.make_async_copy(ref.at[other], half_ref.at[k], in_sem.at[PIECES + k])
+def halves_kernel(sensor_ref, source_ref, outgoing_ref, sem):
+    other = 1 - lax.axis_index("grid")
+    copies = [
+        pltpu.make_async_copy(ref.at[other], outgoing_ref.at[k], sem.at[k])
         for k, ref in enumerate((sensor_ref, source_ref))
     ]
-    pieces = [
-        pltpu.make_async_copy(spectra_ref.at[:, pl.ds(k * rows, rows)], both_ref.at[k], in_sem.at[k])
-        for k in range(PIECES)
-    ]
-    for copy in halves + pieces:
+    for copy in copies:
         copy.start()
-    sends = []
-    for k, copy in enumerate(halves):
+    for copy in copies:
         copy.wait()
-        sends.append(pltpu.make_async_copy(half_ref.at[k], outgoing_ref.at[k], out_sem.at[PIECES + k]))
-        sends[-1].start()
-    for k, copy in enumerate(pieces):
-        copy.wait()
-        sum_ref[k] = both_ref[k, 0] + both_ref[k, 1]
-        sends.append(pltpu.make_async_copy(sum_ref.at[k], packed_ref.at[pl.ds(k * rows, rows)], out_sem.at[k]))
-        sends[-1].start()
-    for copy in sends:
-        copy.wait()
+
+
+def pack_kernel(spectra_ref, packed_ref):
+    packed_ref[...] = spectra_ref[0] + spectra_ref[1]
 
 
 def forms(exact, twice_ref, square_ref, weight, tail, sums_ref):
@@ -201,6 +188,10 @@
     power_ref[pl.ds(1, RANGES, stride=2), :] = power[:, LANES:]
 
 
+def sum_kernel(parts_ref, total_ref):
+    total_ref[...] = jnp.sum(parts_ref[...], 0, keepdims=True)
+
+
 def shape_of(*shape, dtype=jnp.float32):
     return jax.ShapeDtypeStruct(shape, dtype)
 
@@ -212,22 +203,25 @@
     bins = cross_spectra.shape[1]
     mine = lax.axis_index("grid").astype(jnp.int32)
     where = mine.reshape(1)
-    rows = bins * 4 // PIECES
-    packed, outgoing = pl.pallas_call(
+    outgoing = pl.pallas_call(
+        halves_kernel,
+        out_shape=pltpu.VMEM((2, modes, LANES), jnp.float32),
+        in_specs=[HBM, HBM],
+        out_specs=VMEM,
+        scratch_shapes=[pltpu.SemaphoreType.DMA((2,))],
+        cost_estimate=COST,
+        name="halves",
+    )(sensor_modes, source_modes)
+    incoming = lax.ppermute(outgoing, "grid", [(0, 1), (1, 0)])
+    packed = pl.pallas_call(
         pack_kernel,
-        out_shape=[shape_of(bins * 4, LANES), shape_of(2, modes, LANES)],
-        in_specs=[SMEM, ANY, ANY, ANY],
-        out_specs=[ANY] * 2,
-        scratch_shapes=[
-            pltpu.VMEM((PIECES, 2, rows, LANES), jnp.float32),
-            pltpu.VMEM((PIECES, rows, LANES), jnp.float32),
-            pltpu.VMEM((2, modes, LANES), jnp.float32),
-            pltpu.SemaphoreType.DMA((PIECES + 2,)),
-            pltpu.SemaphoreType.DMA((PIECES + 2,)),
-        ],
+        out_shape=shape_of(bins * 4, LANES),
+        in_specs=[VMEM],
+        out_specs=VMEM,
+        cost_estimate=COST,
+        compiler_params=PARAMS,
         name="pack",
-    )(where, cross_spectra.reshape(2, bins * 4, LANES), sensor_modes, source_modes)
-    incoming = lax.ppermute(outgoing, "grid", [(0, 1), (1, 0)])
+    )(cross_spectra.reshape(2, bins * 4, LANES))
     spectra = lax.all_to_all(packed.reshape(bins, 4, LANES), ("freq", "grid"), 0, 0, tiled=True)
     tables = pl.pallas_call(
         functools.partial(denom_kernel, bins),
@@ -269,7 +263,14 @@
         name="numer",
     )(spectra.reshape(-1, LANES), *tables)
     parts = lax.all_to_all(power.reshape(-1, 1, LANES), ("freq", "grid"), 0, 0, tiled=True)
-    return jnp.sum(parts.reshape(-1, LANES), 0, keepdims=True)
+    return pl.pallas_call(
+        sum_kernel,
+        out_shape=shape_of(1, LANES),
+        in_specs=[VMEM],
+        out_specs=VMEM,
+        compiler_params=PARAMS,
+        name="total",
+    )(parts.reshape(-1, LANES))
 
 
 def solution(mesh):

time: 41.6 us -> 41.2 us (level)
  other arithmetic: 0.66 us -> 0 us
  local copies, waits for them, and re-layouts: 0.02 us -> 0.66 us
  waiting for transfers between devices: 8.53 us -> 7.9 us
    reduce_sum x1 -> x0, other arithmetic: 0.66 us -> none  [per_device(): return jnp.sum(parts.reshape(-1, LANES), 0, keepdims=True)]
    unnamed x10 -> x12, local copies, waits for them, and re-layouts: 0.02 us -> 0.66 us
    all_to_all x1, waiting for transfers between devices: 8.53 us -> 7.89 us  [per_device(): lax.all_to_all(packed.reshape(bins, 4, LANES), ('freq', 'grid'), 0, 0, ti...]
    pallas_call x1 -> x3, Pallas kernels: 1.83 us -> 2.16 us  [the longest x1 0.9 us: per_device(): pl.pallas_call(halves_kernel, out_shape=pltpu.VMEM((2, modes, LANES), jnp...]
  transfers between devices with their start and end apart: 2 -> 2, of which waited for: 1 -> 1; matrix products, arithmetic and copies ran while one was open for 0% -> 0% of each run, Pallas kernels for 6% -> 8%
where the time goes in v5:
time: 41.2 us; the launch traced here: 41 us
  blocking collectives  13.7 us (33%)
  starting transfers between devices  12.4 us (30%)
  waiting for transfers between devices  7.9 us (19%)
  Pallas kernels  6.26 us (15%)
  local copies, waits for them, and re-layouts  0.66 us (2%)
    all_to_all x1, blocking collectives, per_device(): lax.all_to_all(power.reshape(-1, 1, LANES), ('freq', 'grid'), 0, 0, tiled...  13.7 us
    all_to_all x1, starting transfers between devices, per_device(): lax.all_to_all(packed.reshape(bins, 4, LANES), ('freq', 'grid'), 0, 0, ti...  7.93 us
    all_to_all x1, waiting for transfers between devices, per_device(): lax.all_to_all(packed.reshape(bins, 4, LANES), ('freq', 'grid'), 0, 0, ti...  7.89 us
    ppermute x1, starting transfers between devices, per_device(): incoming = lax.ppermute(outgoing, 'grid', [(0, 1), (1, 0)])  4.49 us
    pallas_call x1, Pallas kernels, per_device(): pl.pallas_call(functools.partial(denom_kernel, bins), out_shape=[shape_of...  2.37 us
    pallas_call x1, Pallas kernels, per_device(): pl.pallas_call(numer_kernel, out_shape=shape_of(RANGES * 2, LANES), in_sp...  1.73 us
    pallas_call x1, Pallas kernels, per_device(): pl.pallas_call(halves_kernel, out_shape=pltpu.VMEM((2, modes, LANES), jnp...  0.9 us
  transfers between devices with their start and end apart: 2, of which 1 were waited for; matrix products, arithmetic and copies ran while one was open for 0% of the time, Pallas kernels for 8%

profile of v5, /device:TPU:1, one launch (start us, length us, event | category | flops | bytes accessed | tf_op | source)
XLA Modules:
  0.0 41.0 jit_solution(2607527040442378493)
XLA Ops:
  0.0 0.0 copy-start
  0.0 0.9 %halves.1 = f32[2,96,128]{2,1,0:T(8,128)S(1)} custom-call(f32[2,96,128]{2,1,0:T(8,128)} %sensor_ref.3, f32[2,96,128]{2,1,0:T(8,128)} %source_ref.3), custom_call_target="tpu_custom_call" | custom-call | flops 8000000000 | tf_op jit(solution)/shard_map/halves/pallas_call | solution.py:206
  0.9 4.5 %collective-permute-start = (f32[2,96,128]{2,1,0:T(8,128)S(1)}, f32[2,96,128]{2,1,0:T(8,128)S(1)}, u32[]{:S(2)}, u32[]{:S(2)}) collective-permute-start(f32[2,96,128]{2,1,0:T(8,128)S(1)} %halves.1), channel_id=1, source_target_pairs={{0,1},{1,0},{2,3},{3,2},{4,5},{5,4},{6,7},{7,6},{8,9},{9,8},{10,11... | collective-permute-start | bytes 294920 | tf_op jit(solution)/shard_map/ppermute | solution.py:215
  5.4 0.0 copy-done
  5.4 0.7 %pack.1 = f32[512,128]{1,0:T(8,128)} custom-call(f32[2,512,128]{2,1,0:T(8,128)S(1)} %bitcast.11), custom_call_target="tpu_custom_call" | custom-call | flops 8000000000 | tf_op jit(solution)/shard_map/pack/pallas_call | solution.py:216
  6.1 0.0 copy-start.1
  6.1 0.0 copy-start.2
  6.1 7.9 %all-to-all-start = ((f32[128,4,128]{2,1,0:T(4,128)}), f32[128,4,128]{2,1,0:T(4,128)S(1)}, u32[]{:S(2)}, u32[]{:S(2)}) async-start(f32[128,4,128]{2,1,0:T(4,128)} %bitcast.1), calls=%async_computation | async-start | bytes 524288 | tf_op jit(solution)/shard_map/all_to_all | solution.py:225
  14.1 0.0 copy-start.4
  14.1 0.0 copy-start.3
  14.1 0.0 copy-start.5
  14.1 0.0 collective-permute-done.other_ref
  14.1 0.0 copy-done.1
  14.1 0.0 copy-done.2
  14.1 0.6 %copy-done.4 = f32[2,96]{1,0:T(2,128)S(1)} copy-done((f32[2,96]{1,0:T(2,128)S(1)}, f32[2,96]{1,0:T(2,128)}, u32[]{:S(2)}) %copy-start.4) | copy-done | bytes 792
  14.8 0.0 copy-done.3
  14.8 0.0 copy-done.5
  14.8 2.4 %denom.1 = (f32[64,256]{1,0:T(8,128)S(1)}, bf16[256,256]{1,0:T(8,128)(2,1)S(1)}, f32[96,256]{1,0:T(8,128)S(1)}, bf16[256,256]{1,0:T(8,128)(2,1)S(1)}, bf16[192,2...) custom-call(s32[1]{0:T(128)} %bitcast.3.grid_ref, ...), custom_call_target="tpu_custom_call" | custom-call | flops 8000000000 | tf_op jit(solution)/shard_map/denom/pallas_call | solution.py:226
  17.2 7.9 %all-to-all-done = f32[128,4,128]{2,1,0:T(4,128)S(1)} async-done(((f32[128,4,128]{2,1,0:T(4,128)}), f32[128,4,128]{2,1,0:T(4,128)S(1)}, u32[]{:S(2)}, u32[]{:S(2)}) %all-to-all-start) | async-done | bytes 262176 | tf_op jit(solution)/shard_map/all_to_all | solution.py:225
  25.0 1.7 %numer.1 = f32[128,128]{1,0:T(8,128)S(1)} custom-call(f32[512,128]{1,0:T(8,128)S(1)} %bitcast.8, f32[64,256]{1,0:T(8,128)S(1)} %get-tuple-element.14.scale_ref, bf16[256,256]{1,0:T(8,128)(2,1)S(1)} %get-tuple-element.15.weight_ref, f32[96,256]{1,0:T(8,128)S(1)} %get-tuple-element.16.tail_ref, bf16[256,256]{1,0:T(8,128)(2,1)S(1)} %get-tuple-element.17.shapes_ref, ...), custom_call_target="tpu_custom_call" | custom-call | flops 8000000000 | tf_op jit(solution)/shard_map/numer/pallas_call | solution.py:250
  26.8 13.7 %all_to_all.10 = f32[128,1,128]{2,1,0:T(1,128)S(1)} all-to-all(f32[128,1,128]{2,1,0:T(1,128)S(1)} %bitcast.10), channel_id=1, replica_groups=mesh['freq'=64,'grid'=2] {'freq','grid'}, dimensions={0} | all-to-all | bytes 131072 | tf_op jit(solution)/shard_map/all_to_all | solution.py:265
  40.4 0.5 %total.1 = f32[1,128]{1,0:T(1,128)} custom-call(f32[128,128]{1,0:T(8,128)S(1)} %bitcast.9), custom_call_target="tpu_custom_call" | custom-call | tf_op jit(solution)/shard_map/total/pallas_call | solution.py:266
Async XLA Ops:
  0.0 5.4 %copy-start = (f32[2,128,4,128]{3,2,1,0:T(4,128)S(1)}, f32[2,128,4,128]{3,2,1,0:T(4,128)}, u32[]{:S(2)}) copy-start(f32[2,128,4,128]{3,2,1,0:T(4,128)} %param.6) | copy-start | bytes 1572868
  0.9 13.2 %collective-permute-start = (f32[2,96,128]{2,1,0:T(8,128)S(1)}, f32[2,96,128]{2,1,0:T(8,128)S(1)}, u32[]{:S(2)}, u32[]{:S(2)}) collective-permute-start(f32[2,96,128]{2,1,0:T(8,128)S(1)} %halves.1), channel_id=1, source_target_pairs={{0,1},{1,0},{2,3},{3,2},{4,5},{5,4},{6,7},{7,6},{8,9},{9,8},{10,11... | collective-permute-start | bytes 294920 | tf_op jit(solution)/shard_map/ppermute | solution.py:215
  6.1 8.0 %copy-start.1 = (f32[2,96,128]{2,1,0:T(8,128)S(1)}, f32[2,96,128]{2,1,0:T(8,128)}, u32[]{:S(2)}) copy-start(f32[2,96,128]{2,1,0:T(8,128)} %sensor_ref.3) | copy-start | bytes 294916
  6.1 8.0 %copy-start.2 = (f32[2,96,128]{2,1,0:T(8,128)S(1)}, f32[2,96,128]{2,1,0:T(8,128)}, u32[]{:S(2)}) copy-start(f32[2,96,128]{2,1,0:T(8,128)} %source_ref.3) | copy-start | bytes 294916
  6.1 18.9 %all-to-all-start = ((f32[128,4,128]{2,1,0:T(4,128)}), f32[128,4,128]{2,1,0:T(4,128)S(1)}, u32[]{:S(2)}, u32[]{:S(2)}) async-start(f32[128,4,128]{2,1,0:T(4,128)} %bitcast.1), calls=%async_computation | async-start | bytes 524288 | tf_op jit(solution)/shard_map/all_to_all | solution.py:225
  14.1 0.7 %copy-start.4 = (f32[2,96]{1,0:T(2,128)S(1)}, f32[2,96]{1,0:T(2,128)}, u32[]{:S(2)}) copy-start(f32[2,96]{1,0:T(2,128)} %atten_ref.1) | copy-start | bytes 2308
  14.1 0.7 %copy-start.3 = (f32[2,96]{1,0:T(2,128)S(1)}, f32[2,96]{1,0:T(2,128)}, u32[]{:S(2)}) copy-start(f32[2,96]{1,0:T(2,128)} %wave_ref.1) | copy-start | bytes 2308
  14.1 0.7 %copy-start.5 = (s32[2]{0:T(128)S(1)}, s32[2]{0:T(128)}, u32[]{:S(2)}) copy-start(s32[2]{0:T(128)} %counts_ref.1) | copy-start | bytes 28

commit v6 on v5

--- a/solution.py
+++ b/solution.py
@@ -163,15 +163,13 @@
     )
     high, low = split(matrix)
     both = dot(mixed_ref[...], high)
-    product = both[:modes] + both[modes:] + dot(mixed_ref[:modes], low)
+    rest = dot(mixed_ref[:modes], low)
+    product = both[:modes] + (both[modes:] + rest)
     product_high, product_low = split(product)
     shape_high, shape_low = shapes_ref[:LANES], shapes_ref[LANES:]
     whole_ref[...] = jnp.zeros_like(whole_ref)
-    whole_ref[:modes] = (
-        dot(product_high, shape_high, ((1,), (1,)))
-        + dot(product_low, shape_high, ((1,), (1,)))
-        + dot(product_high, shape_low, ((1,), (1,)))
-    )
+    sums = dot(jnp.concatenate([product_high, product_low], 0), shape_high, ((1,), (1,)))
+    whole_ref[:modes] = sums[:modes] + sums[modes:] + dot(product_high, shape_low, ((1,), (1,)))
     square = whole_ref[...]
     turned = square.T
     real_ref[...] = (0.5 * (square + turned))[:modes]

time: 41.2 us -> 41.2 us (level)
  no operation moved by 1% of the time
where the time goes in v6:
time: 41.2 us; the launch traced here: 41 us
  blocking collectives  13.7 us (33%)
  starting transfers between devices  12.4 us (30%)
  waiting for transfers between devices  7.9 us (19%)
  Pallas kernels  6.26 us (15%)
  local copies, waits for them, and re-layouts  0.66 us (2%)
    all_to_all x1, blocking collectives, per_device(): lax.all_to_all(power.reshape(-1, 1, LANES), ('freq', 'grid'), 0, 0, tiled...  13.7 us
    all_to_all x1, starting transfers between devices, per_device(): lax.all_to_all(packed.reshape(bins, 4, LANES), ('freq', 'grid'), 0, 0, ti...  7.93 us
    all_to_all x1, waiting for transfers between devices, per_device(): lax.all_to_all(packed.reshape(bins, 4, LANES), ('freq', 'grid'), 0, 0, ti...  7.89 us
    ppermute x1, starting transfers between devices, per_device(): incoming = lax.ppermute(outgoing, 'grid', [(0, 1), (1, 0)])  4.49 us
    pallas_call x1, Pallas kernels, per_device(): pl.pallas_call(functools.partial(denom_kernel, bins), out_shape=[shape_of...  2.37 us
    pallas_call x1, Pallas kernels, per_device(): pl.pallas_call(numer_kernel, out_shape=shape_of(RANGES * 2, LANES), in_sp...  1.74 us
    pallas_call x1, Pallas kernels, per_device(): pl.pallas_call(halves_kernel, out_shape=pltpu.VMEM((2, modes, LANES), jnp...  0.9 us
  transfers between devices with their start and end apart: 2, of which 1 were waited for; matrix products, arithmetic and copies ran while one was open for 0% of the time, Pallas kernels for 8%

profile of v6, /device:TPU:1, one launch (start us, length us, event | category | flops | bytes accessed | tf_op | source)
XLA Modules:
  0.0 41.0 jit_solution(691131691295218968)
XLA Ops:
  0.0 0.0 copy-start
  0.0 0.9 %halves.1 = f32[2,96,128]{2,1,0:T(8,128)S(1)} custom-call(f32[2,96,128]{2,1,0:T(8,128)} %sensor_ref.3, f32[2,96,128]{2,1,0:T(8,128)} %source_ref.3), custom_call_target="tpu_custom_call" | custom-call | flops 8000000000 | tf_op jit(solution)/shard_map/halves/pallas_call | solution.py:204
  0.9 4.5 %collective-permute-start = (f32[2,96,128]{2,1,0:T(8,128)S(1)}, f32[2,96,128]{2,1,0:T(8,128)S(1)}, u32[]{:S(2)}, u32[]{:S(2)}) collective-permute-start(f32[2,96,128]{2,1,0:T(8,128)S(1)} %halves.1), channel_id=1, source_target_pairs={{0,1},{1,0},{2,3},{3,2},{4,5},{5,4},{6,7},{7,6},{8,9},{9,8},{10,11... | collective-permute-start | bytes 294920 | tf_op jit(solution)/shard_map/ppermute | solution.py:213
  5.4 0.0 copy-done
  5.4 0.7 %pack.1 = f32[512,128]{1,0:T(8,128)} custom-call(f32[2,512,128]{2,1,0:T(8,128)S(1)} %bitcast.11), custom_call_target="tpu_custom_call" | custom-call | flops 8000000000 | tf_op jit(solution)/shard_map/pack/pallas_call | solution.py:214
  6.1 0.0 copy-start.1
  6.1 0.0 copy-start.2
  6.1 7.9 %all-to-all-start = ((f32[128,4,128]{2,1,0:T(4,128)}), f32[128,4,128]{2,1,0:T(4,128)S(1)}, u32[]{:S(2)}, u32[]{:S(2)}) async-start(f32[128,4,128]{2,1,0:T(4,128)} %bitcast.1), calls=%async_computation | async-start | bytes 524288 | tf_op jit(solution)/shard_map/all_to_all | solution.py:223
  14.1 0.0 copy-start.4
  14.1 0.0 copy-start.3
  14.1 0.0 copy-start.5
  14.1 0.0 collective-permute-done.other_ref
  14.1 0.0 copy-done.1
  14.1 0.0 copy-done.2
  14.1 0.6 %copy-done.4 = f32[2,96]{1,0:T(2,128)S(1)} copy-done((f32[2,96]{1,0:T(2,128)S(1)}, f32[2,96]{1,0:T(2,128)}, u32[]{:S(2)}) %copy-start.4) | copy-done | bytes 792
  14.8 0.0 copy-done.3
  14.8 0.0 copy-done.5
  14.8 2.4 %denom.1 = (f32[64,256]{1,0:T(8,128)S(1)}, bf16[256,256]{1,0:T(8,128)(2,1)S(1)}, f32[96,256]{1,0:T(8,128)S(1)}, bf16[256,256]{1,0:T(8,128)(2,1)S(1)}, bf16[192,2...) custom-call(s32[1]{0:T(128)} %bitcast.3.grid_ref, ...), custom_call_target="tpu_custom_call" | custom-call | flops 8000000000 | tf_op jit(solution)/shard_map/denom/pallas_call | solution.py:224
  17.2 7.9 %all-to-all-done = f32[128,4,128]{2,1,0:T(4,128)S(1)} async-done(((f32[128,4,128]{2,1,0:T(4,128)}), f32[128,4,128]{2,1,0:T(4,128)S(1)}, u32[]{:S(2)}, u32[]{:S(2)}) %all-to-all-start) | async-done | bytes 262176 | tf_op jit(solution)/shard_map/all_to_all | solution.py:223
  25.0 1.7 %numer.1 = f32[128,128]{1,0:T(8,128)S(1)} custom-call(f32[512,128]{1,0:T(8,128)S(1)} %bitcast.8, f32[64,256]{1,0:T(8,128)S(1)} %get-tuple-element.14.scale_ref, bf16[256,256]{1,0:T(8,128)(2,1)S(1)} %get-tuple-element.15.weight_ref, f32[96,256]{1,0:T(8,128)S(1)} %get-tuple-element.16.tail_ref, bf16[256,256]{1,0:T(8,128)(2,1)S(1)} %get-tuple-element.17.shapes_ref, ...), custom_call_target="tpu_custom_call" | custom-call | flops 8000000000 | tf_op jit(solution)/shard_map/numer/pallas_call | solution.py:248
  26.8 13.7 %all_to_all.10 = f32[128,1,128]{2,1,0:T(1,128)S(1)} all-to-all(f32[128,1,128]{2,1,0:T(1,128)S(1)} %bitcast.10), channel_id=1, replica_groups=mesh['freq'=64,'grid'=2] {'freq','grid'}, dimensions={0} | all-to-all | bytes 131072 | tf_op jit(solution)/shard_map/all_to_all | solution.py:263
  40.4 0.5 %total.1 = f32[1,128]{1,0:T(1,128)} custom-call(f32[128,128]{1,0:T(8,128)S(1)} %bitcast.9), custom_call_target="tpu_custom_call" | custom-call | tf_op jit(solution)/shard_map/total/pallas_call | solution.py:264
Async XLA Ops:
  0.0 5.4 %copy-start = (f32[2,128,4,128]{3,2,1,0:T(4,128)S(1)}, f32[2,128,4,128]{3,2,1,0:T(4,128)}, u32[]{:S(2)}) copy-start(f32[2,128,4,128]{3,2,1,0:T(4,128)} %param.6) | copy-start | bytes 1572868
  0.9 13.2 %collective-permute-start = (f32[2,96,128]{2,1,0:T(8,128)S(1)}, f32[2,96,128]{2,1,0:T(8,128)S(1)}, u32[]{:S(2)}, u32[]{:S(2)}) collective-permute-start(f32[2,96,128]{2,1,0:T(8,128)S(1)} %halves.1), channel_id=1, source_target_pairs={{0,1},{1,0},{2,3},{3,2},{4,5},{5,4},{6,7},{7,6},{8,9},{9,8},{10,11... | collective-permute-start | bytes 294920 | tf_op jit(solution)/shard_map/ppermute | solution.py:213
  6.1 8.0 %copy-start.1 = (f32[2,96,128]{2,1,0:T(8,128)S(1)}, f32[2,96,128]{2,1,0:T(8,128)}, u32[]{:S(2)}) copy-start(f32[2,96,128]{2,1,0:T(8,128)} %sensor_ref.3) | copy-start | bytes 294916
  6.1 8.0 %copy-start.2 = (f32[2,96,128]{2,1,0:T(8,128)S(1)}, f32[2,96,128]{2,1,0:T(8,128)}, u32[]{:S(2)}) copy-start(f32[2,96,128]{2,1,0:T(8,128)} %source_ref.3) | copy-start | bytes 294916
  6.1 18.9 %all-to-all-start = ((f32[128,4,128]{2,1,0:T(4,128)}), f32[128,4,128]{2,1,0:T(4,128)S(1)}, u32[]{:S(2)}, u32[]{:S(2)}) async-start(f32[128,4,128]{2,1,0:T(4,128)} %bitcast.1), calls=%async_computation | async-start | bytes 524288 | tf_op jit(solution)/shard_map/all_to_all | solution.py:223
  14.1 0.7 %copy-start.4 = (f32[2,96]{1,0:T(2,128)S(1)}, f32[2,96]{1,0:T(2,128)}, u32[]{:S(2)}) copy-start(f32[2,96]{1,0:T(2,128)} %atten_ref.1) | copy-start | bytes 2308
  14.1 0.7 %copy-start.3 = (f32[2,96]{1,0:T(2,128)S(1)}, f32[2,96]{1,0:T(2,128)}, u32[]{:S(2)}) copy-start(f32[2,96]{1,0:T(2,128)} %wave_ref.1) | copy-start | bytes 2308
  14.1 0.7 %copy-start.5 = (s32[2]{0:T(128)S(1)}, s32[2]{0:T(128)}, u32[]{:S(2)}) copy-start(s32[2]{0:T(128)} %counts_ref.1) | copy-start | bytes 28

commit v7 on v5

--- a/solution.py
+++ b/solution.py
@@ -11,6 +11,7 @@
 RANGES = 64
 LANES = 128
 CHUNK = 32
+GROUP = 16
 
 VMEM = pl.BlockSpec(memory_space=pltpu.VMEM)
 HBM = pl.BlockSpec(memory_space=pltpu.HBM)
@@ -48,11 +49,11 @@
 def forms(exact, twice_ref, square_ref, weight, tail, sums_ref):
     modes = tail.shape[0]
     depths = tail.shape[1]
-    for base in range(0, RANGES, CHUNK):
+    before = now = None
+    for base in range(0, RANGES, GROUP):
         left = []
-        before = now = None
-        for j in range(base, base + CHUNK):
-            if j < base + 2:
+        for j in range(base, base + GROUP):
+            if j % CHUNK < 2:
                 later = exact(j)
             else:
                 later = twice_ref[...] * now - square_ref[...] * before
@@ -60,7 +61,7 @@
             high, low = split(now)
             left.append(jnp.concatenate([high, low], 1))
         image = dot(jnp.concatenate(left, 0), weight[...])
-        for k in range(CHUNK):
+        for k in range(GROUP):
             terms = tail[...] * image[k * modes : (k + 1) * modes]
             sums = jnp.sum(terms.reshape(-1, 8, depths), 0)
             row = (base + k) * 8

time: 41.2 us -> 41.2 us (level)
  transfers between devices with their start and end apart: 2 -> 2, of which waited for: 1 -> 1; matrix products, arithmetic and copies ran while one was open for 0% -> 0% of each run, Pallas kernels for 8% -> 7%
where the time goes in v7:
time: 41.2 us; the launch traced here: 41 us
  blocking collectives  13.7 us (33%)
  starting transfers between devices  12.4 us (30%)
  waiting for transfers between devices  7.99 us (19%)
  Pallas kernels  6.15 us (15%)
  local copies, waits for them, and re-layouts  0.66 us (2%)
    all_to_all x1, blocking collectives, per_device(): lax.all_to_all(power.reshape(-1, 1, LANES), ('freq', 'grid'), 0, 0, tiled...  13.7 us
    all_to_all x1, waiting for transfers between devices, per_device(): lax.all_to_all(packed.reshape(bins, 4, LANES), ('freq', 'grid'), 0, 0, ti...  7.99 us
    all_to_all x1, starting transfers between devices, per_device(): lax.all_to_all(packed.reshape(bins, 4, LANES), ('freq', 'grid'), 0, 0, ti...  7.93 us
    ppermute x1, starting transfers between devices, per_device(): incoming = lax.ppermute(outgoing, 'grid', [(0, 1), (1, 0)])  4.49 us
    pallas_call x1, Pallas kernels, per_device(): pl.pallas_call(functools.partial(denom_kernel, bins), out_shape=[shape_of...  2.28 us
    pallas_call x1, Pallas kernels, per_device(): pl.pallas_call(numer_kernel, out_shape=shape_of(RANGES * 2, LANES), in_sp...  1.72 us
    pallas_call x1, Pallas kernels, per_device(): pl.pallas_call(halves_kernel, out_shape=pltpu.VMEM((2, modes, LANES), jnp...  0.9 us
  transfers between devices with their start and end apart: 2, of which 1 were waited for; matrix products, arithmetic and copies ran while one was open for 0% of the time, Pallas kernels for 7%

profile of v7, /device:TPU:1, one launch (start us, length us, event | category | flops | bytes accessed | tf_op | source)
XLA Modules:
  0.0 41.0 jit_solution(17824841345554762840)
XLA Ops:
  0.0 0.0 copy-start
  0.0 0.9 %halves.1 = f32[2,96,128]{2,1,0:T(8,128)S(1)} custom-call(f32[2,96,128]{2,1,0:T(8,128)} %sensor_ref.3, f32[2,96,128]{2,1,0:T(8,128)} %source_ref.3), custom_call_target="tpu_custom_call" | custom-call | flops 8000000000 | tf_op jit(solution)/shard_map/halves/pallas_call | solution.py:207
  0.9 4.5 %collective-permute-start = (f32[2,96,128]{2,1,0:T(8,128)S(1)}, f32[2,96,128]{2,1,0:T(8,128)S(1)}, u32[]{:S(2)}, u32[]{:S(2)}) collective-permute-start(f32[2,96,128]{2,1,0:T(8,128)S(1)} %halves.1), channel_id=1, source_target_pairs={{0,1},{1,0},{2,3},{3,2},{4,5},{5,4},{6,7},{7,6},{8,9},{9,8},{10,11... | collective-permute-start | bytes 294920 | tf_op jit(solution)/shard_map/ppermute | solution.py:216
  5.4 0.0 copy-done
  5.4 0.7 %pack.1 = f32[512,128]{1,0:T(8,128)} custom-call(f32[2,512,128]{2,1,0:T(8,128)S(1)} %bitcast.11), custom_call_target="tpu_custom_call" | custom-call | flops 8000000000 | tf_op jit(solution)/shard_map/pack/pallas_call | solution.py:217
  6.1 0.0 copy-start.1
  6.1 0.0 copy-start.2
  6.1 7.9 %all-to-all-start = ((f32[128,4,128]{2,1,0:T(4,128)}), f32[128,4,128]{2,1,0:T(4,128)S(1)}, u32[]{:S(2)}, u32[]{:S(2)}) async-start(f32[128,4,128]{2,1,0:T(4,128)} %bitcast.1), calls=%async_computation | async-start | bytes 524288 | tf_op jit(solution)/shard_map/all_to_all | solution.py:226
  14.1 0.0 copy-start.4
  14.1 0.0 copy-start.3
  14.1 0.0 copy-start.5
  14.1 0.0 collective-permute-done.other_ref
  14.1 0.0 copy-done.1
  14.1 0.0 copy-done.2
  14.1 0.6 %copy-done.4 = f32[2,96]{1,0:T(2,128)S(1)} copy-done((f32[2,96]{1,0:T(2,128)S(1)}, f32[2,96]{1,0:T(2,128)}, u32[]{:S(2)}) %copy-start.4) | copy-done | bytes 792
  14.8 0.0 copy-done.3
  14.8 0.0 copy-done.5
  14.8 2.3 %denom.1 = (f32[64,256]{1,0:T(8,128)S(1)}, bf16[256,256]{1,0:T(8,128)(2,1)S(1)}, f32[96,256]{1,0:T(8,128)S(1)}, bf16[256,256]{1,0:T(8,128)(2,1)S(1)}, bf16[192,2...) custom-call(s32[1]{0:T(128)} %bitcast.3.grid_ref, ...), custom_call_target="tpu_custom_call" | custom-call | flops 8000000000 | tf_op jit(solution)/shard_map/denom/pallas_call | solution.py:227
  17.1 8.0 %all-to-all-done = f32[128,4,128]{2,1,0:T(4,128)S(1)} async-done(((f32[128,4,128]{2,1,0:T(4,128)}), f32[128,4,128]{2,1,0:T(4,128)S(1)}, u32[]{:S(2)}, u32[]{:S(2)}) %all-to-all-start) | async-done | bytes 262176 | tf_op jit(solution)/shard_map/all_to_all | solution.py:226
  25.0 1.7 %numer.1 = f32[128,128]{1,0:T(8,128)S(1)} custom-call(f32[512,128]{1,0:T(8,128)S(1)} %bitcast.8, f32[64,256]{1,0:T(8,128)S(1)} %get-tuple-element.14.scale_ref, bf16[256,256]{1,0:T(8,128)(2,1)S(1)} %get-tuple-element.15.weight_ref, f32[96,256]{1,0:T(8,128)S(1)} %get-tuple-element.16.tail_ref, bf16[256,256]{1,0:T(8,128)(2,1)S(1)} %get-tuple-element.17.shapes_ref, ...), custom_call_target="tpu_custom_call" | custom-call | flops 8000000000 | tf_op jit(solution)/shard_map/numer/pallas_call | solution.py:251
  26.8 13.7 %all_to_all.10 = f32[128,1,128]{2,1,0:T(1,128)S(1)} all-to-all(f32[128,1,128]{2,1,0:T(1,128)S(1)} %bitcast.10), channel_id=1, replica_groups=mesh['freq'=64,'grid'=2] {'freq','grid'}, dimensions={0} | all-to-all | bytes 131072 | tf_op jit(solution)/shard_map/all_to_all | solution.py:266
  40.4 0.5 %total.1 = f32[1,128]{1,0:T(1,128)} custom-call(f32[128,128]{1,0:T(8,128)S(1)} %bitcast.9), custom_call_target="tpu_custom_call" | custom-call | tf_op jit(solution)/shard_map/total/pallas_call | solution.py:267
Async XLA Ops:
  0.0 5.4 %copy-start = (f32[2,128,4,128]{3,2,1,0:T(4,128)S(1)}, f32[2,128,4,128]{3,2,1,0:T(4,128)}, u32[]{:S(2)}) copy-start(f32[2,128,4,128]{3,2,1,0:T(4,128)} %param.6) | copy-start | bytes 1572868
  0.9 13.2 %collective-permute-start = (f32[2,96,128]{2,1,0:T(8,128)S(1)}, f32[2,96,128]{2,1,0:T(8,128)S(1)}, u32[]{:S(2)}, u32[]{:S(2)}) collective-permute-start(f32[2,96,128]{2,1,0:T(8,128)S(1)} %halves.1), channel_id=1, source_target_pairs={{0,1},{1,0},{2,3},{3,2},{4,5},{5,4},{6,7},{7,6},{8,9},{9,8},{10,11... | collective-permute-start | bytes 294920 | tf_op jit(solution)/shard_map/ppermute | solution.py:216
  6.1 8.0 %copy-start.1 = (f32[2,96,128]{2,1,0:T(8,128)S(1)}, f32[2,96,128]{2,1,0:T(8,128)}, u32[]{:S(2)}) copy-start(f32[2,96,128]{2,1,0:T(8,128)} %sensor_ref.3) | copy-start | bytes 294916
  6.1 8.0 %copy-start.2 = (f32[2,96,128]{2,1,0:T(8,128)S(1)}, f32[2,96,128]{2,1,0:T(8,128)}, u32[]{:S(2)}) copy-start(f32[2,96,128]{2,1,0:T(8,128)} %source_ref.3) | copy-start | bytes 294916
  6.1 18.9 %all-to-all-start = ((f32[128,4,128]{2,1,0:T(4,128)}), f32[128,4,128]{2,1,0:T(4,128)S(1)}, u32[]{:S(2)}, u32[]{:S(2)}) async-start(f32[128,4,128]{2,1,0:T(4,128)} %bitcast.1), calls=%async_computation | async-start | bytes 524288 | tf_op jit(solution)/shard_map/all_to_all | solution.py:226
  14.1 0.7 %copy-start.4 = (f32[2,96]{1,0:T(2,128)S(1)}, f32[2,96]{1,0:T(2,128)}, u32[]{:S(2)}) copy-start(f32[2,96]{1,0:T(2,128)} %atten_ref.1) | copy-start | bytes 2308
  14.1 0.7 %copy-start.3 = (f32[2,96]{1,0:T(2,128)S(1)}, f32[2,96]{1,0:T(2,128)}, u32[]{:S(2)}) copy-start(f32[2,96]{1,0:T(2,128)} %wave_ref.1) | copy-start | bytes 2308
  14.1 0.7 %copy-start.5 = (s32[2]{0:T(128)S(1)}, s32[2]{0:T(128)}, u32[]{:S(2)}) copy-start(s32[2]{0:T(128)} %counts_ref.1) | copy-start | bytes 28
